TPU v7x, 512 devices: a whole 4x8x8 slice. The times are simulated.
512 devices in a mesh: space: 64 (over y_lo, z, x), tensor: 8 (over y_hi, core).
Axes of the slice: x: 4, y: 8 (y_hi: 4, y_lo: 2; y = y_hi * 2 + y_lo), z: 8, core: 2. Of those that a mesh axis runs over, the one named last changes fastest.
Arguments:
- tokens: float32 [2, 128, 128, 2048], P(None, 'space', None, 'tensor'), may hold values from -6 to 6
- in_gain: float32 [2048], replicated, may hold values from 0.25 to 1.75
- w_inner: bfloat16 [2048, 3072], P(None, 'tensor'), may hold values from -0.125 to 0.125
- w_bc: bfloat16 [2048, 256], replicated, may hold values from -0.03125 to 0.03125
- w_step: bfloat16 [2048, 48], P(None, 'tensor'), may hold values from -0.125 to 0.125
- step_bias: float32 [48], P('tensor'), may hold values from -3 to 0
- decay_rate: float32 [48], P('tensor'), may hold values from 0.02 to 2
- skip: float32 [48], P('tensor'), may hold values from 0.5 to 2
- norm_gain: float32 [3072], P('tensor'), may hold values from 0.25 to 1.75
- w_out: bfloat16 [3072, 2048], P('tensor'), may hold values from -0.109375 to 0.109375
Outputs:
- mixed: bfloat16 [2, 128, 128, 2048], P(None, 'space', None, 'tensor')
All inputs are finite; a program needn't handle non-finite values.
Results may differ from a plain program's by a relative error of at most 0.011.
Values may be sent and summed in bfloat16 or wider, within the bound.
No kernel may reach another device: no remote copies, remote signals or barrier semaphores. Data moves between devices by JAX's collectives and lax.ppermute only.
A program may use at most 64 MiB of HBM per device.

v0:
```python
import jax
import jax.numpy as jnp
from jax import lax
from jax.sharding import PartitionSpec as P

HEAD_DIM = 64
STATE = 128
NORM_HEADS = 6


EPS = 1e-05


def kernel(logdecay):
    running = jnp.cumsum(logdecay, axis=-1)
    length = logdecay.shape[-1]
    place = jnp.arange(length)
    lower = place[:, None] >= place[None, :]
    upper = place[:, None] <= place[None, :]
    later = running[..., :, None] - running[..., None, :]
    shifted = running - logdecay
    earlier = shifted[..., None, :] - shifted[..., :, None]
    forward = jnp.exp(jnp.where(lower, later, -jnp.inf))
    backward = jnp.exp(jnp.where(upper, earlier, -jnp.inf))
    return forward + backward


def scan_grid(values, maps, logdecay, along_rows):
    heads = logdecay.shape[-1]
    in_map = maps[..., :STATE]
    out_map = maps[..., STATE:]
    split_values = values.reshape(values.shape[:3] + (heads, HEAD_DIM))
    if along_rows:
        scores = jnp.einsum("ialn,iamn->ialm", out_map, in_map, preferred_element_type=jnp.float32)
        decays = jnp.moveaxis(logdecay.astype(jnp.float32), 3, 2)
    else:
        scores = jnp.einsum("ilan,iman->ialm", out_map, in_map, preferred_element_type=jnp.float32)
        decays = jnp.transpose(logdecay.astype(jnp.float32), (0, 2, 3, 1))
    weights = (scores[:, :, None] * kernel(decays)).astype(jnp.bfloat16)
    if along_rows:
        result = jnp.einsum(
            "iahlm,iamhp->ialhp", weights, split_values, preferred_element_type=jnp.float32
        )
    else:
        result = jnp.einsum(
            "iahlm,imahp->ilahp", weights, split_values, preferred_element_type=jnp.float32
        )
    return result.reshape(values.shape)


def on_device(
    tokens, in_gain, w_inner, w_bc, w_step, step_bias, decay_rate, skip, norm_gain, w_out
):
    whole = lax.all_gather(tokens.astype(jnp.bfloat16), "tensor", axis=3, tiled=True)
    rounded = whole.astype(jnp.float32)
    scale = lax.rsqrt(jnp.mean(rounded * rounded, axis=-1, keepdims=True) + EPS)
    normed = (rounded * scale * in_gain).astype(jnp.bfloat16)
    inner = jnp.einsum("irwd,dc->irwc", normed, w_inner, preferred_element_type=jnp.float32).astype(
        jnp.bfloat16
    )
    maps = jnp.einsum("irwd,dc->irwc", normed, w_bc, preferred_element_type=jnp.float32).astype(
        jnp.bfloat16
    )
    step = jax.nn.softplus(
        jnp.einsum("irwd,dc->irwc", normed, w_step, preferred_element_type=jnp.float32) + step_bias
    )
    logdecay = (-decay_rate * step).astype(jnp.bfloat16)
    heads_local = w_step.shape[1]
    lead = inner.shape[:3]
    value = (
        (inner.reshape(lead + (heads_local, HEAD_DIM)).astype(jnp.float32) * step[..., None])
        .reshape(inner.shape)
        .astype(jnp.bfloat16)
    )
    col_value = lax.all_to_all(value, "space", split_axis=2, concat_axis=1, tiled=True)
    col_maps = lax.all_to_all(maps, "space", split_axis=2, concat_axis=1, tiled=True)
    col_decay = lax.all_to_all(logdecay, "space", split_axis=2, concat_axis=1, tiled=True)
    column_out = scan_grid(col_value, col_maps, col_decay, False).astype(jnp.bfloat16)
    column_back = lax.all_to_all(column_out, "space", split_axis=1, concat_axis=2, tiled=True)
    row_out = scan_grid(value, maps, logdecay, True)
    skip_wide = jnp.repeat(skip, HEAD_DIM)
    total = row_out + column_back.astype(jnp.float32) + skip_wide * inner.astype(jnp.float32)
    group = NORM_HEADS * HEAD_DIM
    grouped = total.reshape(lead + (inner.shape[3] // group, group))
    norm_scale = lax.rsqrt(jnp.mean(grouped * grouped, axis=-1, keepdims=True) + EPS)
    gated = ((grouped * norm_scale).reshape(inner.shape) * norm_gain).astype(jnp.bfloat16)
    partial_out = jnp.einsum("irwc,cd->irwd", gated, w_out, preferred_element_type=jnp.float32)
    mixer = lax.psum_scatter(partial_out, "tensor", scatter_dimension=3, tiled=True)
    return (tokens + mixer).astype(jnp.bfloat16)


def solution(mesh):
    return jax.shard_map(
        on_device,
        mesh=mesh,
        in_specs=(
            P(None, "space", None, "tensor"),
            P(),
            P(None, "tensor"),
            P(),
            P(None, "tensor"),
            P("tensor"),
            P("tensor"),
            P("tensor"),
            P("tensor"),
            P("tensor", None),
        ),
        out_specs=P(None, "space", None, "tensor"),
        check_vma=False,
    )
```

profile of v0, /device:TPU:19, one launch (start us, length us, event | category | flops | bytes accessed | tf_op | source)
XLA Modules:
  0.0 218.5 jit_solution(5063790395113188788)
XLA Ops:
  6.6 1.9 convert_element_type.76
  9.2 45.6 %all-gather.2.cloned.1.call-done = bf16[2,2,128,2048]{3,2,1,0:T(8,128)(2,1)} async-done(((bf16[2,2,128,256]{3,2,1,0:T(8,128)(2,1)}), bf16[2,2,128,2048]{3,2,1,0:T(8,128)(2,1)}) %all-gather.2.cloned.1.call-update) | async-done | bytes 2097168 | tf_op jit(solution)/shard_map/all_gather | solution.py:54
  54.7 2.2 %fusion = f32[2,2,128]{2,1,0:T(2,128)S(1)} fusion(bf16[2,2,128,2048]{3,2,1,0:T(8,128)(2,1)} %all-gather.2.cloned.1.call-done), kind=kLoop, calls=%fused_computation.2 | loop fusion | flops 3145216 | bytes 2099200 | tf_op jit(solution)/shard_map/reduce_sum | solution.py:56
  58.6 12.8 %all-to-all-start.2 = ((bf16[2,2,128,6]{3,1,0,2:T(2,128)(2,1)}), bf16[2,2,128,6]{3,1,0,2:T(2,128)(2,1)S(1)}, u32[]{:S(2)}, u32[]{:S(2)}) async-start(bf16[2,2,128,6]{3,1,0,2:T(2,128)(2,1)} %copy.52), calls=%async_computation.2 | async-start | bytes 262144 | tf_op jit(solution)/shard_map/all_to_all | solution.py:77
  71.5 2.4 %convolution_convert_fusion.1 = bf16[2,2,128,256]{3,2,1,0:T(8,128)(2,1)S(1)} fusion(bf16[2,2,128,2048]{3,2,1,0:T(8,128)(2,1)} %all-gather.2.cloned.1.call-done, f32[2048]{0:T(1024)S(1)} %copy-done.13, f32[2,2,128]{2,1,0:T(2,128)S(1)} %add_rsqrt_fusion.1, bf16[2048,256]{1,0:T(8,128)(2,1)S(1)} %copy-done.11), kind=kOutput, calls=%fused_computation.14 | convolution fusion | flops 541196288 | bytes 3418112 | tf_op jit(solution)/shard_map/irwd,dc->irwc/dot_general | solution.py:61
  74.8 5.6 %all-to-all-done.2 = bf16[2,2,128,6]{3,1,0,2:T(2,128)(2,1)S(1)} async-done(((bf16[2,2,128,6]{3,1,0,2:T(2,128)(2,1)}), bf16[2,2,128,6]{3,1,0,2:T(2,128)(2,1)S(1)}, u32[]{:S(2)}, u32[]{:S(2)}) %all-to-all-start.2) | async-done | bytes 6176 | tf_op jit(solution)/shard_map/all_to_all | solution.py:77
  80.5 6.1 %all-to-all-start.1 = ((bf16[2,2,128,256]{3,1,0,2:T(2,128)(2,1)}), bf16[2,2,128,256]{3,1,0,2:T(2,128)(2,1)S(1)}, u32[]{:S(2)}, u32[]{:S(2)}) async-start(bf16[2,2,128,256]{3,1,0,2:T(2,128)(2,1)} %copy.48), calls=%async_computation.1 | async-start | bytes 524288 | tf_op jit(solution)/shard_map/all_to_all | solution.py:76
  87.4 1.2 copy.44
  88.5 4.4 %multiply_convert_fusion.5 = (bf16[2,2,128,384]{3,2,1,0:T(8,128)(2,1)S(1)}, f32[2,2,128,384]{3,2,1,0:T(8,128)}) fusion(f32[2,2,128,384]{3,2,1,0:T(8,128)} %copy.44, bf16[2048,384]{1,0:T(8,128)(2,1)} %param.12, bf16[2,2,128,2048]{3,2,1,0:T(8,128)(2,1)} %all-gather.2.cloned.1.call-done, f32[2048]{0:T(1024)S(1)} %copy-done.13, ...), kind=kOutput, calls=%fused_computation.34 | convolution fusion | flops 810287104 | bytes 5646336 | tf_op jit(solution)/shard_map/irwd,dc->irwc/dot_general | solution.py:58
  94.1 2.0 all-to-all-done.1
  96.1 8.8 %all-to-all-start = ((bf16[2,2,128,384]{3,1,0,2:T(2,128)(2,1)}), bf16[2,2,128,384]{3,1,0,2:T(2,128)(2,1)S(1)}, u32[]{:S(2)}, u32[]{:S(2)}) async-start(bf16[2,2,128,384]{3,1,0,2:T(2,128)(2,1)} %copy.46), calls=%async_computation | async-start | bytes 786432 | tf_op jit(solution)/shard_map/all_to_all | solution.py:75
  108.4 6.6 %all-to-all-done = bf16[2,2,128,384]{3,1,0,2:T(2,128)(2,1)S(1)} async-done(((bf16[2,2,128,384]{3,1,0,2:T(2,128)(2,1)}), bf16[2,2,128,384]{3,1,0,2:T(2,128)(2,1)S(1)}, u32[]{:S(2)}, u32[]{:S(2)}) %all-to-all-start) | async-done | bytes 393248 | tf_op jit(solution)/shard_map/all_to_all | solution.py:75
  115.3 1.6 reshape.67
  116.9 2.5 %convolution_convert_fusion = bf16[2,2,6,64,128]{4,3,2,1,0:T(8,128)(2,1)S(1)} fusion(bf16[2,128,2,6,64]{4,3,2,1,0:T(8,128)(2,1)} %reshape.67, f32[2,2,6,128]{3,2,1,0:T(8,128)} %bitcast_subtract_fusion, f32[2,2,6,128]{3,2,1,0:T(8,128)} %copy-done.3, f32[2,2,128,128]{3,2,1,0:T(8,128)S(1)} %fusion.40, pred[128,128]{1,0:T(8,128)(4,1)} %get-tuple-element.14, ...), kind=kOutput, calls=%fused_computation.13 | convolution fusion | flops 53280768 | bytes 1105920 | tf_op jit(solution)/shard_map/iahlm,imahp->ilahp/dot_general | solution.py:45
  120.5 10.5 %all-to-all-start.3 = ((bf16[2,128,2,384]{3,2,0,1:T(2,128)(2,1)}), bf16[2,128,2,384]{3,2,0,1:T(2,128)(2,1)S(1)}, u32[]{:S(2)}, u32[]{:S(2)}) async-start(bf16[2,128,2,384]{3,2,0,1:T(2,128)(2,1)} %copy.58), calls=%async_computation.3 | async-start | bytes 786432 | tf_op jit(solution)/shard_map/all_to_all | solution.py:79
  131.6 1.2 reduce_window_sum.17
  133.0 2.0 fusion.17
  135.1 1.4 copy.62
  136.5 4.8 %all-to-all-done.3 = bf16[2,128,2,384]{3,2,0,1:T(2,128)(2,1)S(1)} async-done(((bf16[2,128,2,384]{3,2,0,1:T(2,128)(2,1)}), bf16[2,128,2,384]{3,2,0,1:T(2,128)(2,1)S(1)}, u32[]{:S(2)}, u32[]{:S(2)}) %all-to-all-start.3) | async-done | bytes 393248 | tf_op jit(solution)/shard_map/all_to_all | solution.py:79
  142.2 1.4 reshape.68
  143.7 1.6 multiply_reduce_fusion
  145.3 3.3 %fusion.3 = f32[2,2,128,2048]{3,2,1,0:T(8,128)} fusion(bf16[384,2048]{1,0:T(8,128)(2,1)S(1)} %copy-done, f32[2,2,128,384]{3,2,1,0:T(8,128)S(1)} %get-tuple-element.6, f32[384]{0:T(512)S(1)} %copy-done.7, f32[2,2,128]{2,1,0:T(2,128)S(1)} %add_rsqrt_fusion), kind=kOutput, calls=%fused_computation.5 | convolution fusion | flops 805896192 | bytes 6557184 | tf_op jit(solution)/shard_map/irwc,cd->irwd/dot_general | solution.py:87
  148.6 61.3 %reduce-scatter.2.cloned.1.call-done = f32[2,2,128,256]{3,2,1,0:T(8,128)} async-done(((f32[2,2,128,2048]{3,2,1,0:T(8,128)}), f32[2,2,128,256]{3,2,1,0:T(8,128)}) %reduce-scatter.2.cloned.1.call-update) | async-done | bytes 524304 | tf_op jit(solution)/shard_map/reduce_scatter | solution.py:88
  209.8 1.8 add_convert_fusion
  (63 shorter events, 12.0 us)
Async XLA Ops:
  6.5 138.7 %copy-start = (bf16[384,2048]{1,0:T(8,128)(2,1)S(1)}, bf16[384,2048]{1,0:T(8,128)(2,1)}, u32[]{:S(2)}) copy-start(bf16[384,2048]{1,0:T(8,128)(2,1)} %param.19) | copy-start | bytes 4718596
  6.5 50.4 %copy-start.13 = (f32[2048]{0:T(1024)S(1)}, f32[2048]{0:T(1024)}, u32[]{:S(2)}) copy-start(f32[2048]{0:T(1024)} %param.11) | copy-start | bytes 24580
  6.5 50.4 %copy-start.14 = (f32[6]{0:T(128)S(1)}, f32[6]{0:T(128)}, u32[]{:S(2)}) copy-start(f32[6]{0:T(128)} %param.15) | copy-start | bytes 76
  6.5 50.5 %copy-start.12 = (bf16[2048,6]{0,1:T(8,128)(2,1)S(1)}, bf16[2048,6]{0,1:T(8,128)(2,1)}, u32[]{:S(2)}) copy-start(bf16[2048,6]{0,1:T(8,128)(2,1)} %param.14) | copy-start | bytes 73732
  6.5 48.2 %all-gather.2.cloned.1.call-start = ((), (), s32[]{:S(2)}) async-start(), calls=%async_computation.5 | async-start | bytes 2359296 | tf_op jit(solution)/shard_map/all_gather | solution.py:54
  9.2 48.7 %copy-start.8 = (f32[6]{0:T(128)}, f32[6]{0:T(128)S(1)}, u32[]{:S(2)}) copy-start(f32[6]{0:T(128)S(1)} %neg.11) | copy-start | bytes 76
  54.7 2.3 %copy-start.1 = (bf16[2,2,128,2048]{3,2,1,0:T(8,128)(2,1)S(1)}, bf16[2,2,128,2048]{3,2,1,0:T(8,128)(2,1)}, u32[]{:S(2)}) copy-start(bf16[2,2,128,2048]{3,2,1,0:T(8,128)(2,1)} %all-gather.2.cloned.1.call-done) | copy-start | bytes 6291460
  57.0 14.4 %copy-start.11 = (bf16[2048,256]{1,0:T(8,128)(2,1)S(1)}, bf16[2048,256]{1,0:T(8,128)(2,1)}, u32[]{:S(2)}) copy-start(bf16[2048,256]{1,0:T(8,128)(2,1)} %param.13) | copy-start | bytes 3145732
  58.6 21.8 %all-to-all-start.2 = ((bf16[2,2,128,6]{3,1,0,2:T(2,128)(2,1)}), bf16[2,2,128,6]{3,1,0,2:T(2,128)(2,1)S(1)}, u32[]{:S(2)}, u32[]{:S(2)}) async-start(bf16[2,2,128,6]{3,1,0,2:T(2,128)(2,1)} %copy.52), calls=%async_computation.2 | async-start | bytes 262144 | tf_op jit(solution)/shard_map/all_to_all | solution.py:77
  71.5 15.1 %copy-start.10 = (f32[6]{0:T(128)S(1)}, f32[6]{0:T(128)}, u32[]{:S(2)}) copy-start(f32[6]{0:T(128)} %param.17) | copy-start | bytes 76
  80.5 15.6 %all-to-all-start.1 = ((bf16[2,2,128,256]{3,1,0,2:T(2,128)(2,1)}), bf16[2,2,128,256]{3,1,0,2:T(2,128)(2,1)S(1)}, u32[]{:S(2)}, u32[]{:S(2)}) async-start(bf16[2,2,128,256]{3,1,0,2:T(2,128)(2,1)} %copy.48), calls=%async_computation.1 | async-start | bytes 524288 | tf_op jit(solution)/shard_map/all_to_all | solution.py:76
  96.1 18.9 %all-to-all-start = ((bf16[2,2,128,384]{3,1,0,2:T(2,128)(2,1)}), bf16[2,2,128,384]{3,1,0,2:T(2,128)(2,1)S(1)}, u32[]{:S(2)}, u32[]{:S(2)}) async-start(bf16[2,2,128,384]{3,1,0,2:T(2,128)(2,1)} %copy.46), calls=%async_computation | async-start | bytes 786432 | tf_op jit(solution)/shard_map/all_to_all | solution.py:75
  107.2 7.8 %copy-start.3 = (f32[2,2,6,128]{3,2,1,0:T(8,128)}, f32[2,2,6,128]{3,2,1,0:T(8,128)S(1)}, u32[]{:S(2)}) copy-start(f32[2,2,6,128]{3,2,1,0:T(8,128)S(1)} %reduce_window_sum.18) | copy-start | bytes 36868
  119.4 11.9 %copy-start.9 = (f32[6]{0:T(128)S(1)}, f32[6]{0:T(128)}, u32[]{:S(2)}) copy-start(f32[6]{0:T(128)} %copy-done.8) | copy-start | bytes 76
  119.4 13.6 %copy-start.4 = (pred[128,128]{1,0:T(8,128)(4,1)S(1)}, pred[128,128]{1,0:T(8,128)(4,1)}, u32[]{:S(2)}) copy-start(pred[128,128]{1,0:T(8,128)(4,1)} %get-tuple-element.14) | copy-start | bytes 49156
  119.4 13.6 %copy-start.5 = (pred[128,128]{1,0:T(8,128)(4,1)S(1)}, pred[128,128]{1,0:T(8,128)(4,1)}, u32[]{:S(2)}) copy-start(pred[128,128]{1,0:T(8,128)(4,1)} %get-tuple-element.15) | copy-start | bytes 49156
  120.5 20.8 %all-to-all-start.3 = ((bf16[2,128,2,384]{3,2,0,1:T(2,128)(2,1)}), bf16[2,128,2,384]{3,2,0,1:T(2,128)(2,1)S(1)}, u32[]{:S(2)}, u32[]{:S(2)}) async-start(bf16[2,128,2,384]{3,2,0,1:T(2,128)(2,1)} %copy.58), calls=%async_computation.3 | async-start | bytes 786432 | tf_op jit(solution)/shard_map/all_to_all | solution.py:79
  131.0 78.8 %reduce-scatter.2.cloned.1.call-start = ((), (), s32[]{:S(2)}) async-start(), calls=%async_computation.6 | async-start | bytes 4718592 | tf_op jit(solution)/shard_map/reduce_scatter | solution.py:88
  141.9 1.7 copy-start.6
  143.7 1.6 copy-start.7
  148.6 61.3 %copy-start.2 = (f32[2,2,128,256]{3,2,1,0:T(8,128)S(1)}, f32[2,2,128,256]{3,2,1,0:T(8,128)}, u32[]{:S(2)}) copy-start(f32[2,2,128,256]{3,2,1,0:T(8,128)} %param.10) | copy-start | bytes 1572868
Sparse Core Ops, SparseCore 0:
  9.5 45.2 all-gather.1
  148.7 61.0 reduce-scatter.1
where the time goes:
time: 219 us; the launch traced here: 218 us
  waiting for transfers between devices  126 us (58%)
  starting transfers between devices  38.4 us (18%)
  matrix products  15.8 us (7%)
  between operations  13.7 us (6%)
  local copies, waits for them, and re-layouts  12.8 us (6%)
  other arithmetic  11.9 us (5%)
    reduce_scatter x1, waiting for transfers between devices, on_device(): lax.psum_scatter(partial_out, 'tensor', scatter_dimension=3, tiled=True)  61.3 us
    all_gather x1, waiting for transfers between devices, on_device(): lax.all_gather(tokens.astype(jnp.bfloat16), 'tensor', axis=3, tiled=True)  45.6 us
    all_to_all x1, starting transfers between devices, on_device(): lax.all_to_all(logdecay, 'space', split_axis=2, concat_axis=1, tiled=True)  12.8 us
    all_to_all x1, starting transfers between devices, on_device(): lax.all_to_all(column_out, 'space', split_axis=1, concat_axis=2, tiled=True)  10.5 us
    all_to_all x1, starting transfers between devices, on_device(): lax.all_to_all(value, 'space', split_axis=2, concat_axis=1, tiled=True)  8.77 us
    all_to_all x1, waiting for transfers between devices, on_device(): lax.all_to_all(value, 'space', split_axis=2, concat_axis=1, tiled=True)  6.57 us
    all_to_all x1, starting transfers between devices, on_device(): lax.all_to_all(maps, 'space', split_axis=2, concat_axis=1, tiled=True)  6.09 us
    all_to_all x1, waiting for transfers between devices, on_device(): lax.all_to_all(logdecay, 'space', split_axis=2, concat_axis=1, tiled=True)  5.64 us
  transfers between devices with their start and end apart: 6, of which 6 were waited for; matrix products, arithmetic and copies ran while one was open for 9% of the time, Pallas kernels for 0%

commit v1 on v0

v1 whole, which is shorter than its diff:
```python
import jax
import jax.numpy as jnp
from jax import lax
from jax.experimental import pallas as pl
from jax.experimental.pallas import tpu as pltpu
from jax.sharding import PartitionSpec as P

HEAD_DIM = 64
STATE = 128
LANES = 128
EPS = 1e-05
BF16 = jnp.bfloat16
F32 = jnp.float32


def dot(a, b, dims=((1,), (0,))):
    return lax.dot_general(a, b, (dims, ((), ())), preferred_element_type=F32)


def one_hot(rows, cols, target):
    t = lax.broadcasted_iota(jnp.int32, (rows, 1), 0)
    q = lax.broadcasted_iota(jnp.int32, (rows, cols), 1)
    return jnp.where(target(t) == q, 1.0, 0.0).astype(BF16)


def block(chip, core, part):
    chips = 4
    offset = (((chip + 2 * chips) & (chips - 1)) * 2 + core) * part
    return pl.ds(pl.multiple_of(offset, part), part)


def position():
    place = lax.axis_index("tensor")
    core = place & 1
    return place >> 1, core, 1 - 2 * core


def spots():
    y_hi, core, way = position()
    other = 1 - core
    early = [(y_hi, core), (y_hi - way, core), (y_hi + way, core)]
    early += [(y_hi, other), (y_hi + way, other), (y_hi - way, other)]
    return early, [(y_hi + 2, core), (y_hi + 2, other)]


def scaled(pieces, gain_ref, squares, y_ref):
    step_rows = 64
    part = pieces[0].shape[1]
    gains = [gain_ref[k : k + 1, :] for k in range(len(pieces))]

    def some(n, carry):
        rows = pl.ds(pl.multiple_of(n * step_rows, step_rows), step_rows)
        total = squares(rows)
        for k, ref in enumerate(pieces):
            x = ref[rows, :].astype(F32)
            y_ref[rows, k * part : (k + 1) * part] = (x * gains[k]).astype(BF16)
            x = x * x
            for m in range(part // LANES):
                total += x[:, m * LANES : (m + 1) * LANES]
        carry[rows, :] = total

    def loop(out_ref):
        @pl.loop(0, y_ref.shape[0] // step_rows)
        def _(n):
            some(n, out_ref)

    return loop


def prepare_kernel(*refs):
    gain_ref, w_inner_hbm, w_bc_hbm, w_step_ref, bias_ref, rate_ref = refs[:6]
    outs, small_ref, sems = (refs[6:9], refs[9:12]), refs[12], refs[13]
    channels, states = w_inner_hbm.shape[1], w_bc_hbm.shape[1]
    heads = w_step_ref.shape[0]
    part = outs[0][2].shape[1]
    copies = []
    for (w_ref, step_ref, gains_ref), blocks in zip(outs, spots()):
        for k, (chip, side) in enumerate(blocks):
            for source, lanes in ((w_inner_hbm, (0, channels)), (w_bc_hbm, (channels, states))):
                copy = pltpu.make_async_copy(
                    source.at[block(chip, side, part), :],
                    w_ref.at[pl.ds(k * part, part), pl.ds(*lanes)],
                    sems.at[len(copies)],
                )
                copy.start()
                copies.append(copy)
    small_ref[...] = jnp.zeros_like(small_ref)
    small_ref[0:1, :heads] = bias_ref[...]
    small_ref[1:2, :heads] = rate_ref[...]
    for (w_ref, step_ref, gains_ref), blocks in zip(outs, spots()):
        step_ref[...] = jnp.zeros_like(step_ref)
        gains_ref[...] = jnp.zeros_like(gains_ref)
        for k, (chip, side) in enumerate(blocks):
            step_ref[:heads, k * part : (k + 1) * part] = w_step_ref[:, block(chip, side, part)]
            row = ((chip + 8) & 3) * 4 + side * 2
            for m in range(part // LANES):
                gains_ref[k : k + 1, m * LANES : (m + 1) * LANES] = gain_ref[pl.ds(row + m, 1), :]
    for copy in copies:
        copy.wait()


def first_kernel(*refs):
    pieces = refs[:6]
    w_ref, step_ref, gain_ref = refs[6:9]
    acc_ref, squares_ref, y_ref = refs[9:]
    wide = w_ref.shape[1]
    scaled(pieces, gain_ref, lambda rows: jnp.zeros((64, LANES), F32), y_ref)(squares_ref)
    y = y_ref[...]
    acc_ref[:, :wide] = dot(y, w_ref[...])
    acc_ref[:, wide:] = dot(y, step_ref[...], ((1,), (1,)))


def project_kernel(*refs):
    pieces = refs[:2]
    w_ref, step_ref, gain_ref, small_ref, acc_ref, squares_ref = refs[2:8]
    send_ref, inner_ref, value_ref, side_ref = refs[8:12]
    y_ref, total_ref = refs[12:]
    patches = pieces[0].shape[0]
    channels = inner_ref.shape[1]
    wide = w_ref.shape[1]
    states = wide - channels
    scaled(pieces, gain_ref, lambda rows: squares_ref[rows, :], y_ref)(total_ref)
    mean = jnp.sum(total_ref[...], axis=-1, keepdims=True) / (4 * y_ref.shape[1])
    scale = lax.rsqrt(mean + EPS)
    y = y_ref[...]
    raw = acc_ref[:, wide:] + dot(y, step_ref[...], ((1,), (1,)))
    step = jax.nn.softplus(raw * scale + small_ref[0:1, :])
    side_ref[:, states:] = (-small_ref[1:2, :] * step).astype(BF16)
    maps = acc_ref[:, channels:wide] + dot(y, w_ref[:, channels:])
    side_ref[:, :states] = (maps * scale).astype(BF16)
    inner = ((acc_ref[:, :channels] + dot(y, w_ref[:, :channels])) * scale).astype(BF16)
    inner_ref[...] = inner
    left = lax.broadcasted_iota(jnp.int32, (patches, LANES), 1) < HEAD_DIM
    for k in range(channels // LANES):
        widened = jnp.where(left, step[:, 2 * k : 2 * k + 1], step[:, 2 * k + 1 : 2 * k + 2])
        at = slice(k * LANES, (k + 1) * LANES)
        value_ref[:, at] = (inner[:, at].astype(F32) * widened).astype(BF16)
    order = one_hot(patches, patches, lambda t: ((t & 3) << 7) + ((t >> 3) << 1) + ((t >> 2) & 1))
    send_ref[:, :channels] = dot(order, value_ref[...]).astype(BF16)
    send_ref[:, channels:] = dot(order, side_ref[...]).astype(BF16)


def scan(value, side):
    length = value.shape[0]
    heads = value.shape[1] // HEAD_DIM
    in_map, out_map = side[:, :STATE], side[:, STATE : 2 * STATE]
    decay = side[:, 2 * STATE :]
    scores = dot(out_map, in_map, ((1,), (1,)))
    t = lax.broadcasted_iota(jnp.int32, (length, length), 0)
    r = lax.broadcasted_iota(jnp.int32, (length, length), 1)
    lower = jnp.where(t >= r, 1.0, 0.0).astype(BF16)
    upper = jnp.where(t <= r, 1.0, 0.0).astype(BF16)
    unit = jnp.where(t == r, 1.0, 0.0).astype(BF16)
    running = dot(lower, decay)
    across = dot(decay, upper, ((0,), (0,)))
    shifted = running - decay.astype(F32)
    shifted_across = across - dot(decay, unit, ((0,), (0,)))
    doubled = jnp.where(t == r, 2.0 * scores, scores)
    below = r <= t
    outs = []
    for h in range(heads):
        later = running[:, h : h + 1] - across[h : h + 1, :]
        earlier = shifted_across[h : h + 1, :] - shifted[:, h : h + 1]
        weights = doubled * jnp.exp(jnp.where(below, jnp.where(t == r, 0.0, later), earlier))
        outs.append(
            dot(weights.astype(BF16), value[:, h * HEAD_DIM : (h + 1) * HEAD_DIM])
        )
    return jnp.concatenate(outs, axis=1)


def row_kernel(value_ref, side_ref, inner_ref, skip_ref, out_ref):
    length = LANES
    for row in range(value_ref.shape[0] // length):
        at = pl.ds(row * length, length)
        out_ref[at, :] = (
            scan(value_ref[at, :], side_ref[at, :])
            + skip_ref[...] * inner_ref[at, :].astype(F32)
        )


def column_kernel(recv_ref, back_ref, sorted_ref, outs_ref):
    rows = recv_ref.shape[0]
    channels = back_ref.shape[1]
    length = rows // 4
    order = one_hot(
        rows, rows, lambda t: (((t & 127) >> 1) << 3) + ((t >> 7) << 1) + (t & 1)
    )
    sorted_ref[...] = dot(order, recv_ref[...]).astype(BF16)
    for n in range(4):
        at = pl.ds(n * length, length)
        outs_ref[at, :] = scan(sorted_ref[at, :channels], sorted_ref[at, channels:]).astype(BF16)
    back = one_hot(rows, rows, lambda t: (((t >> 1) & 3) << 7) + ((t >> 3) << 1) + (t & 1))
    back_ref[...] = dot(back, outs_ref[...]).astype(BF16)


def output_kernel(back_ref, row_ref, gain_ref, w_ref, *out_refs):
    y_hi, core, way = position()
    patches = row_ref.shape[0]
    order = one_hot(
        patches, patches, lambda t: (((t & 127) >> 1) << 3) + ((t & 1) << 2) + (t >> 7)
    )
    total = row_ref[...] + dot(order, back_ref[...])
    scale = lax.rsqrt(jnp.mean(total * total, axis=-1, keepdims=True) + EPS)
    gated = (total * scale * gain_ref[...]).astype(BF16)
    part = out_refs[0].shape[1]
    spots = [(2, 1 - core), (way, 1 - core), (-way, 1 - core), (0, 1 - core)]
    spots += [(2, core), (-way, core), (way, core), (0, core)]
    for ref, (chip, side) in zip(out_refs, spots):
        ref[...] = dot(gated, w_ref[:, block(y_hi + chip, side, part)]).astype(ref.dtype)


def call(body, outs, args, flops, scratch=(), in_hbm=()):
    size = sum(a.size * a.dtype.itemsize for a in args)
    size += sum(o.size * o.dtype.itemsize for o in outs)
    return pl.pallas_call(
        body,
        out_shape=outs,
        in_specs=[
            pl.BlockSpec(memory_space=pltpu.HBM if n in in_hbm else pltpu.VMEM)
            for n in range(len(args))
        ],
        out_specs=[pl.BlockSpec(memory_space=pltpu.VMEM)] * len(outs),
        scratch_shapes=list(scratch),
        cost_estimate=pl.CostEstimate(flops=flops, bytes_accessed=size, transcendentals=0),
        compiler_params=pltpu.CompilerParams(vmem_limit_bytes=24 * 1024 * 1024),
    )(*args)


def shape(dims, dtype):
    return jax.ShapeDtypeStruct(dims, dtype)


def hop(x, sign):
    pairs = []
    for t in range(8):
        way = sign * (1 - 2 * (t & 1))
        pairs.append((t, (t + 2 * way) % 8))
    return lax.ppermute(x, "tensor", pairs)


def swap(x):
    return lax.ppermute(x, "tensor", [(t, t ^ 1) for t in range(8)])


def layer(
    tokens, in_gain, w_inner, w_bc, w_step, step_bias, decay_rate, skip, norm_gain, w_out
):
    images, rows, width, part = tokens.shape
    patches = images * rows * width
    channels = w_inner.shape[1]
    gain = in_gain.reshape(-1, LANES)
    bias = step_bias[None, :]
    rate = decay_rate[None, :]
    skip_wide = jnp.repeat(skip, HEAD_DIM)[None, :]
    out_gain = norm_gain[None, :]
    flat = tokens.reshape(patches, part)
    space = lax.axis_size("space")

    def exchange(x):
        y = x.reshape(space, -1, x.shape[-1])
        y = lax.all_to_all(y, "space", split_axis=0, concat_axis=0, tiled=True)
        return y.reshape(x.shape)

    x = flat.astype(BF16)
    ahead, behind = hop(x, 1), hop(x, -1)
    wide = channels + 2 * STATE
    counts = [6 * part, 2 * part]
    orders = [
        o
        for n in counts
        for o in (shape((n, wide), BF16), shape((LANES, n), BF16), shape((8, part), F32))
    ]
    prepared = call(
        prepare_kernel,
        orders + [shape((8, LANES), F32)],
        [gain, w_inner, w_bc, w_step.T, bias, rate],
        4 * 10**9,
        [pltpu.SemaphoreType.DMA((16,))],
        in_hbm=(1, 2),
    )
    ahead, *prepared = lax.optimization_barrier((ahead, *prepared))
    across = hop(ahead, 1)
    early = [x, ahead, behind, swap(x), swap(ahead), swap(behind)]
    started = call(
        first_kernel,
        [shape((patches, wide + LANES), F32), shape((patches, LANES), F32)],
        early + prepared[:3],
        4 * 10**9,
        [pltpu.VMEM((patches, counts[0]), BF16)],
    )
    across, *started = lax.optimization_barrier((across, *started))
    pieces = [across, swap(across)]
    wide += LANES
    dims = [(patches, wide), (patches, channels), (patches, channels), (patches, wide - channels)]
    send, inner, value, side = call(
        project_kernel,
        [shape(d, BF16) for d in dims],
        pieces + prepared[3:] + started,
        2 * 10**9,
        [pltpu.VMEM((patches, counts[1]), BF16), pltpu.VMEM((patches, LANES), F32)],
    )
    got = exchange(send)
    (back,) = call(
        column_kernel,
        [shape((patches, channels), BF16)],
        [got],
        8 * 10**8,
        [pltpu.VMEM((patches, wide), BF16), pltpu.VMEM((patches, channels), BF16)],
    )
    back = exchange(back)
    (row,) = call(
        row_kernel, [shape((patches, channels), F32)], [value, side, inner, skip_wide], 8 * 10**8
    )
    pieces = call(
        output_kernel,
        [shape((patches, part), BF16)] * 4 + [shape((patches, part), F32)] * 4,
        [back, row, out_gain, w_out],
        2 * patches * channels * 2048,
    )
    give, keep = pieces[:4], pieces[4:]
    taken = [swap(g).astype(F32) for g in give]
    sums = [k + t for k, t in zip(keep, taken)]
    far = hop(sums[0].astype(BF16), 1)
    near = hop(sums[1].astype(BF16), -1)
    last = hop((sums[2] + far.astype(F32)).astype(BF16), 1)
    total = flat + sums[3] + near.astype(F32) + last.astype(F32)
    return total.astype(BF16).reshape(tokens.shape)


def solution(mesh):
    return jax.shard_map(
        layer,
        mesh=mesh,
        in_specs=(
            P(None, "space", None, "tensor"),
            P(),
            P(None, "tensor"),
            P(),
            P(None, "tensor"),
            P("tensor"),
            P("tensor"),
            P("tensor"),
            P("tensor"),
            P("tensor", None),
        ),
        out_specs=P(None, "space", None, "tensor"),
        check_vma=False,
    )
```

time: 219 us -> 140 us (0.64)
  the two profiles are of different devices: /device:TPU:19 before, /device:TPU:54 now
where the time goes in v1:
time: 140 us; the launch traced here: 139 us
  starting transfers between devices  48.5 us (35%)
  blocking collectives  35 us (25%)
  waiting for transfers between devices  33.8 us (24%)
  Pallas kernels  12.4 us (9%)
  local copies, waits for them, and re-layouts  6.65 us (5%)
  other arithmetic  2.13 us (2%)
    all_to_all x1, blocking collectives, exchange(): y = lax.all_to_all(y, 'space', split_axis=0, concat_axis=0, tiled=True)  35 us
    ppermute x6, waiting for transfers between devices, hop(): return lax.ppermute(x, 'tensor', pairs)  22 us
    ppermute x8, starting transfers between devices, swap(): return lax.ppermute(x, 'tensor', [(t, t ^ 1) for t in range(8)])  20.9 us
    ppermute x6, starting transfers between devices, hop(): return lax.ppermute(x, 'tensor', pairs)  19.6 us
    pallas_call x6, Pallas kernels, call(): pl.pallas_call(body, out_shape=outs, in_specs=[pl.BlockSpec(memory_space=...  12.4 us
    all_to_all x1, waiting for transfers between devices, exchange(): y = lax.all_to_all(y, 'space', split_axis=0, concat_axis=0, tiled=True)  10.3 us
    all_to_all x1, starting transfers between devices, exchange(): y = lax.all_to_all(y, 'space', split_axis=0, concat_axis=0, tiled=True)  7.98 us
    unnamed x24, local copies, waits for them, and re-layouts  6.5 us
  transfers between devices with their start and end apart: 15, of which 5 were waited for; matrix products, arithmetic and copies ran while one was open for 0% of the time, Pallas kernels for 4%

profile of v1, /device:TPU:54, one launch (start us, length us, event | category | flops | bytes accessed | tf_op | source)
XLA Modules:
  0.0 138.7 jit_solution(13415232063102009885)
XLA Ops:
  1.1 1.9 %collective-permute-start = (bf16[512,256]{1,0:T(8,128)(2,1)S(1)}, bf16[512,256]{1,0:T(8,128)(2,1)S(1)}, u32[]{:S(2)}, u32[]{:S(2)}) collective-permute-start(bf16[512,256]{1,0:T(8,128)(2,1)S(1)} %bitcast_convert_fusion.refs_0_), channel_id=1, source_target_pairs={{0,2},{1,7},{2,4},{3,1},{4,6},{5,3},{6,0},{7,5},{8,10},{9,15},{10,... | collective-permute-start | bytes 786440 | tf_op jit(solution)/shard_map/ppermute | solution.py:238
  3.0 4.8 %collective-permute-start.2 = (bf16[512,256]{1,0:T(8,128)(2,1)S(1)}, bf16[512,256]{1,0:T(8,128)(2,1)S(1)}, u32[]{:S(2)}, u32[]{:S(2)}) collective-permute-start(bf16[512,256]{1,0:T(8,128)(2,1)S(1)} %bitcast_convert_fusion.refs_0_), channel_id=1, source_target_pairs={{0,6},{1,3},{2,0},{3,5},{4,2},{5,7},{6,4},{7,1},{8,14},{9,11},{10,... | collective-permute-start | bytes 786440 | tf_op jit(solution)/shard_map/ppermute | solution.py:238
  7.8 2.4 %collective-permute-start.3 = (bf16[512,256]{1,0:T(8,128)(2,1)S(1)}, bf16[512,256]{1,0:T(8,128)(2,1)S(1)}, u32[]{:S(2)}, u32[]{:S(2)}) collective-permute-start(bf16[512,256]{1,0:T(8,128)(2,1)S(1)} %bitcast_convert_fusion.refs_0_), channel_id=1, source_target_pairs={{0,1},{1,0},{2,3},{3,2},{4,5},{5,4},{6,7},{7,6},{8,9},{9,8},{10,11... | collective-permute-start | bytes 786440 | tf_op jit(solution)/shard_map/ppermute | solution.py:242
  16.1 3.1 %collective-permute-start.4 = (bf16[512,256]{1,0:T(8,128)(2,1)S(1)}, bf16[512,256]{1,0:T(8,128)(2,1)S(1)}, u32[]{:S(2)}, u32[]{:S(2)}) collective-permute-start(bf16[512,256]{1,0:T(8,128)(2,1)S(1)} %collective-permute-done.refs_1_), channel_id=1, source_target_pairs={{0,1},{1,0},{2,3},{3,2},{4,5},{5,4},{6,7},{7,6},{8,9},{9,8},{10,11... | collective-permute-start | bytes 786440 | tf_op jit(solution)/shard_map/ppermute | solution.py:242
  19.3 1.9 %collective-permute-start.5 = (bf16[512,256]{1,0:T(8,128)(2,1)S(1)}, bf16[512,256]{1,0:T(8,128)(2,1)S(1)}, u32[]{:S(2)}, u32[]{:S(2)}) collective-permute-start(bf16[512,256]{1,0:T(8,128)(2,1)S(1)} %collective-permute-done.2.refs_2_), channel_id=1, source_target_pairs={{0,1},{1,0},{2,3},{3,2},{4,5},{5,4},{6,7},{7,6},{8,9},{9,8},{10,11... | collective-permute-start | bytes 786440 | tf_op jit(solution)/shard_map/ppermute | solution.py:242
  21.2 2.0 %collective-permute-start.1 = (bf16[512,256]{1,0:T(8,128)(2,1)S(1)}, bf16[512,256]{1,0:T(8,128)(2,1)S(1)}, u32[]{:S(2)}, u32[]{:S(2)}) collective-permute-start(bf16[512,256]{1,0:T(8,128)(2,1)S(1)} %collective-permute-done.refs_1_), channel_id=1, source_target_pairs={{0,2},{1,7},{2,4},{3,1},{4,6},{5,3},{6,0},{7,5},{8,10},{9,15},{10,... | collective-permute-start | bytes 786440 | tf_op jit(solution)/shard_map/ppermute | solution.py:238
  23.3 2.3 %shard_map.101 = (f32[512,768]{1,0:T(8,128)S(1)}, f32[512,128]{1,0:T(8,128)S(1)}) custom-call(bf16[512,256]{1,0:T(8,128)(2,1)S(1)} %bitcast_convert_fusion.refs_0_, bf16[512,256]{1,0:T(8,128)(2,1)S(1)} %collective-permute-done.refs_1_, bf16[512,256]{1,0:T(8,128)(2,1)S(1)} %collective-permute-done.2.refs_2_, ...), custom_call_target="tpu_custom_call" | custom-call | flops 4000000000 | bytes 5775360 | tf_op jit(solution)/shard_map/pallas_call | solution.py:215
  25.6 9.0 %collective-permute-done.1.refs_0_ = bf16[512,256]{1,0:T(8,128)(2,1)S(1)} collective-permute-done((bf16[512,256]{1,0:T(8,128)(2,1)S(1)}, bf16[512,256]{1,0:T(8,128)(2,1)S(1)}, u32[]{:S(2)}, u32[]{:S(2)}) %collective-permute-start.1) | collective-permute-done | bytes 262176 | tf_op jit(solution)/shard_map/ppermute | solution.py:238
  34.6 1.9 %collective-permute-start.6 = (bf16[512,256]{1,0:T(8,128)(2,1)S(1)}, bf16[512,256]{1,0:T(8,128)(2,1)S(1)}, u32[]{:S(2)}, u32[]{:S(2)}) collective-permute-start(bf16[512,256]{1,0:T(8,128)(2,1)S(1)} %collective-permute-done.1.refs_0_), channel_id=1, source_target_pairs={{0,1},{1,0},{2,3},{3,2},{4,5},{5,4},{6,7},{7,6},{8,9},{9,8},{10,11... | collective-permute-start | bytes 786440 | tf_op jit(solution)/shard_map/ppermute | solution.py:242
  38.0 1.9 %shard_map.102 = (bf16[512,768]{1,0:T(8,128)(2,1)S(1)}, bf16[512,384]{1,0:T(8,128)(2,1)S(1)}, bf16[512,384]{1,0:T(8,128)(2,1)S(1)}, bf16[512,384]{1,0:T(8,128)(2,1)S(1)}) custom-call(bf16[512,256]{1,0:T(8,128)(2,1)S(1)} %collective-permute-done.1.refs_0_, bf16[512,256]{1,0:T(8,128)(2,1)S(1)} %collective-permute-done.6.refs_1_, ...), custom_call_target="tpu_custom_call" | custom-call | flops 2000000000 | bytes 5124096 | tf_op jit(solution)/shard_map/pallas_call | solution.py:215
  39.9 35.0 %all_to_all.10 = bf16[64,8,768]{2,1,0:T(8,128)(2,1)S(1)} all-to-all(bf16[64,8,768]{2,1,0:T(8,128)(2,1)S(1)} %bitcast.18), channel_id=1, replica_groups=mesh['space'=64,'tensor'=8] {'space'}, dimensions={0} | all-to-all | bytes 1572864 | tf_op jit(solution)/shard_map/all_to_all | solution.py:261
  74.9 4.0 %shard_map.103 = bf16[512,384]{1,0:T(8,128)(2,1)} custom-call(bf16[512,768]{1,0:T(8,128)(2,1)S(1)} %bitcast.19), custom_call_target="tpu_custom_call" | custom-call | flops 800000000 | bytes 1179648 | tf_op jit(solution)/shard_map/pallas_call | solution.py:215
  78.9 8.0 %all-to-all-start.1 = ((bf16[64,8,384]{2,1,0:T(8,128)(2,1)}), bf16[64,8,384]{2,1,0:T(8,128)(2,1)S(1)}, u32[]{:S(2)}, u32[]{:S(2)}) async-start(bf16[64,8,384]{2,1,0:T(8,128)(2,1)} %bitcast.7), calls=%async_computation.1 | async-start | bytes 786432 | tf_op jit(solution)/shard_map/all_to_all | solution.py:261
  88.2 2.1 %shard_map.104.row_ref = f32[512,384]{1,0:T(8,128)S(1)} custom-call(bf16[512,384]{1,0:T(8,128)(2,1)S(1)} %get-tuple-element.58.value_ref, bf16[512,384]{1,0:T(8,128)(2,1)S(1)} %copy-done.8, bf16[512,384]{1,0:T(8,128)(2,1)S(1)} %get-tuple-element.60.inner_ref, f32[1,384]{1,0:T(1,128)S(1)} %broadcast_in_dim_reshape.3.skip_ref), custom_call_target="tpu_custom_call" | custom-call | flops 800000000 | bytes 1967616 | tf_op jit(solution)/shard_map/pallas_call | solution.py:215
  90.3 10.3 %all-to-all-done.1 = bf16[64,8,384]{2,1,0:T(8,128)(2,1)S(1)} async-done(((bf16[64,8,384]{2,1,0:T(8,128)(2,1)}), bf16[64,8,384]{2,1,0:T(8,128)(2,1)S(1)}, u32[]{:S(2)}, u32[]{:S(2)}) %all-to-all-start.1) | async-done | bytes 393248 | tf_op jit(solution)/shard_map/all_to_all | solution.py:261
  102.2 1.9 %collective-permute-start.11 = (bf16[512,256]{1,0:T(8,128)(2,1)S(1)}, bf16[512,256]{1,0:T(8,128)(2,1)S(1)}, u32[]{:S(2)}, u32[]{:S(2)}) collective-permute-start(bf16[512,256]{1,0:T(8,128)(2,1)S(1)} %get-tuple-element.68), channel_id=1, source_target_pairs={{0,1},{1,0},{2,3},{3,2},{4,5},{5,4},{6,7},{7,6},{8,9},{9,8},{10,11... | collective-permute-start | bytes 786440 | tf_op jit(solution)/shard_map/ppermute | solution.py:242
  104.2 2.4 %collective-permute-start.8 = (bf16[512,256]{1,0:T(8,128)(2,1)S(1)}, bf16[512,256]{1,0:T(8,128)(2,1)S(1)}, u32[]{:S(2)}, u32[]{:S(2)}) collective-permute-start(bf16[512,256]{1,0:T(8,128)(2,1)S(1)} %get-tuple-element.64), channel_id=1, source_target_pairs={{0,1},{1,0},{2,3},{3,2},{4,5},{5,4},{6,7},{7,6},{8,9},{9,8},{10,11... | collective-permute-start | bytes 786440 | tf_op jit(solution)/shard_map/ppermute | solution.py:242
  106.6 1.9 %collective-permute-start.10 = (bf16[512,256]{1,0:T(8,128)(2,1)S(1)}, bf16[512,256]{1,0:T(8,128)(2,1)S(1)}, u32[]{:S(2)}, u32[]{:S(2)}) collective-permute-start(bf16[512,256]{1,0:T(8,128)(2,1)S(1)} %get-tuple-element.66), channel_id=1, source_target_pairs={{0,1},{1,0},{2,3},{3,2},{4,5},{5,4},{6,7},{7,6},{8,9},{9,8},{10,11... | collective-permute-start | bytes 786440 | tf_op jit(solution)/shard_map/ppermute | solution.py:242
  108.6 2.9 %collective-permute-start.12 = (bf16[512,256]{1,0:T(8,128)(2,1)S(1)}, bf16[512,256]{1,0:T(8,128)(2,1)S(1)}, u32[]{:S(2)}, u32[]{:S(2)}) collective-permute-start(bf16[512,256]{1,0:T(8,128)(2,1)S(1)} %add_convert_fusion.1), channel_id=1, source_target_pairs={{0,2},{1,7},{2,4},{3,1},{4,6},{5,3},{6,0},{7,5},{8,10},{9,15},{10,... | collective-permute-start | bytes 786440 | tf_op jit(solution)/shard_map/ppermute | solution.py:238
  111.5 5.3 %collective-permute-start.7 = (bf16[512,256]{1,0:T(8,128)(2,1)S(1)}, bf16[512,256]{1,0:T(8,128)(2,1)S(1)}, u32[]{:S(2)}, u32[]{:S(2)}) collective-permute-start(bf16[512,256]{1,0:T(8,128)(2,1)S(1)} %get-tuple-element.62), channel_id=1, source_target_pairs={{0,1},{1,0},{2,3},{3,2},{4,5},{5,4},{6,7},{7,6},{8,9},{9,8},{10,11... | collective-permute-start | bytes 786440 | tf_op jit(solution)/shard_map/ppermute | solution.py:242
  116.8 2.2 %collective-permute-start.9 = (bf16[512,256]{1,0:T(8,128)(2,1)S(1)}, bf16[512,256]{1,0:T(8,128)(2,1)S(1)}, u32[]{:S(2)}, u32[]{:S(2)}) collective-permute-start(bf16[512,256]{1,0:T(8,128)(2,1)S(1)} %add_convert_fusion.2), channel_id=1, source_target_pairs={{0,6},{1,3},{2,0},{3,5},{4,2},{5,7},{6,4},{7,1},{8,14},{9,11},{10,... | collective-permute-start | bytes 786440 | tf_op jit(solution)/shard_map/ppermute | solution.py:238
  119.1 5.8 %collective-permute-start.13 = (bf16[512,256]{1,0:T(8,128)(2,1)S(1)}, bf16[512,256]{1,0:T(8,128)(2,1)S(1)}, u32[]{:S(2)}, u32[]{:S(2)}) collective-permute-start(bf16[512,256]{1,0:T(8,128)(2,1)S(1)} %add_convert_fusion), channel_id=1, source_target_pairs={{0,2},{1,7},{2,4},{3,1},{4,6},{5,3},{6,0},{7,5},{8,10},{9,15},{10,... | collective-permute-start | bytes 786440 | tf_op jit(solution)/shard_map/ppermute | solution.py:238
  124.9 8.2 %collective-permute-done.9 = bf16[512,256]{1,0:T(8,128)(2,1)S(1)} collective-permute-done((bf16[512,256]{1,0:T(8,128)(2,1)S(1)}, bf16[512,256]{1,0:T(8,128)(2,1)S(1)}, u32[]{:S(2)}, u32[]{:S(2)}) %collective-permute-start.9) | collective-permute-done | bytes 262176 | tf_op jit(solution)/shard_map/ppermute | solution.py:238
  133.1 4.8 %collective-permute-done.13 = bf16[512,256]{1,0:T(8,128)(2,1)S(1)} collective-permute-done((bf16[512,256]{1,0:T(8,128)(2,1)S(1)}, bf16[512,256]{1,0:T(8,128)(2,1)S(1)}, u32[]{:S(2)}, u32[]{:S(2)}) %collective-permute-start.13) | collective-permute-done | bytes 262176 | tf_op jit(solution)/shard_map/ppermute | solution.py:238
  (45 shorter events, 12.4 us)
Async XLA Ops:
  1.1 15.1 %collective-permute-start = (bf16[512,256]{1,0:T(8,128)(2,1)S(1)}, bf16[512,256]{1,0:T(8,128)(2,1)S(1)}, u32[]{:S(2)}, u32[]{:S(2)}) collective-permute-start(bf16[512,256]{1,0:T(8,128)(2,1)S(1)} %bitcast_convert_fusion.refs_0_), channel_id=1, source_target_pairs={{0,2},{1,7},{2,4},{3,1},{4,6},{5,3},{6,0},{7,5},{8,10},{9,15},{10,... | collective-permute-start | bytes 786440 | tf_op jit(solution)/shard_map/ppermute | solution.py:238
  3.0 16.3 %collective-permute-start.2 = (bf16[512,256]{1,0:T(8,128)(2,1)S(1)}, bf16[512,256]{1,0:T(8,128)(2,1)S(1)}, u32[]{:S(2)}, u32[]{:S(2)}) collective-permute-start(bf16[512,256]{1,0:T(8,128)(2,1)S(1)} %bitcast_convert_fusion.refs_0_), channel_id=1, source_target_pairs={{0,6},{1,3},{2,0},{3,5},{4,2},{5,7},{6,4},{7,1},{8,14},{9,11},{10,... | collective-permute-start | bytes 786440 | tf_op jit(solution)/shard_map/ppermute | solution.py:238
  7.8 15.4 %collective-permute-start.3 = (bf16[512,256]{1,0:T(8,128)(2,1)S(1)}, bf16[512,256]{1,0:T(8,128)(2,1)S(1)}, u32[]{:S(2)}, u32[]{:S(2)}) collective-permute-start(bf16[512,256]{1,0:T(8,128)(2,1)S(1)} %bitcast_convert_fusion.refs_0_), channel_id=1, source_target_pairs={{0,1},{1,0},{2,3},{3,2},{4,5},{5,4},{6,7},{7,6},{8,9},{9,8},{10,11... | collective-permute-start | bytes 786440 | tf_op jit(solution)/shard_map/ppermute | solution.py:242
  10.2 1.4 %copy-start = (bf16[2048,384]{1,0:T(8,128)(2,1)S(1)}, bf16[2048,384]{1,0:T(8,128)(2,1)}, u32[]{:S(2)}) copy-start(bf16[2048,384]{1,0:T(8,128)(2,1)} %refs_1_.1) | copy-start | bytes 4718596
  11.6 1.2 copy-start.2
  12.9 0.8 copy-start.3
  16.1 7.1 %collective-permute-start.4 = (bf16[512,256]{1,0:T(8,128)(2,1)S(1)}, bf16[512,256]{1,0:T(8,128)(2,1)S(1)}, u32[]{:S(2)}, u32[]{:S(2)}) collective-permute-start(bf16[512,256]{1,0:T(8,128)(2,1)S(1)} %collective-permute-done.refs_1_), channel_id=1, source_target_pairs={{0,1},{1,0},{2,3},{3,2},{4,5},{5,4},{6,7},{7,6},{8,9},{9,8},{10,11... | collective-permute-start | bytes 786440 | tf_op jit(solution)/shard_map/ppermute | solution.py:242
  19.3 4.0 %collective-permute-start.5 = (bf16[512,256]{1,0:T(8,128)(2,1)S(1)}, bf16[512,256]{1,0:T(8,128)(2,1)S(1)}, u32[]{:S(2)}, u32[]{:S(2)}) collective-permute-start(bf16[512,256]{1,0:T(8,128)(2,1)S(1)} %collective-permute-done.2.refs_2_), channel_id=1, source_target_pairs={{0,1},{1,0},{2,3},{3,2},{4,5},{5,4},{6,7},{7,6},{8,9},{9,8},{10,11... | collective-permute-start | bytes 786440 | tf_op jit(solution)/shard_map/ppermute | solution.py:242
  21.2 13.4 %collective-permute-start.1 = (bf16[512,256]{1,0:T(8,128)(2,1)S(1)}, bf16[512,256]{1,0:T(8,128)(2,1)S(1)}, u32[]{:S(2)}, u32[]{:S(2)}) collective-permute-start(bf16[512,256]{1,0:T(8,128)(2,1)S(1)} %collective-permute-done.refs_1_), channel_id=1, source_target_pairs={{0,2},{1,7},{2,4},{3,1},{4,6},{5,3},{6,0},{7,5},{8,10},{9,15},{10,... | collective-permute-start | bytes 786440 | tf_op jit(solution)/shard_map/ppermute | solution.py:238
  34.6 3.4 %collective-permute-start.6 = (bf16[512,256]{1,0:T(8,128)(2,1)S(1)}, bf16[512,256]{1,0:T(8,128)(2,1)S(1)}, u32[]{:S(2)}, u32[]{:S(2)}) collective-permute-start(bf16[512,256]{1,0:T(8,128)(2,1)S(1)} %collective-permute-done.1.refs_0_), channel_id=1, source_target_pairs={{0,1},{1,0},{2,3},{3,2},{4,5},{5,4},{6,7},{7,6},{8,9},{9,8},{10,11... | collective-permute-start | bytes 786440 | tf_op jit(solution)/shard_map/ppermute | solution.py:242
  39.9 39.0 %copy-start.7 = (bf16[512,384]{1,0:T(8,128)(2,1)}, bf16[512,384]{1,0:T(8,128)(2,1)S(1)}, u32[]{:S(2)}) copy-start(bf16[512,384]{1,0:T(8,128)(2,1)S(1)} %get-tuple-element.59.side_ref) | copy-start | bytes 1179652
  74.9 12.0 %copy-start.11 = (f32[6]{0:T(128)S(1)}, f32[6]{0:T(128)}, u32[]{:S(2)}) copy-start(f32[6]{0:T(128)} %param.17) | copy-start | bytes 76
  74.9 12.2 %copy-start.10 = (f32[384]{0:T(512)S(1)}, f32[384]{0:T(512)}, u32[]{:S(2)}) copy-start(f32[384]{0:T(512)} %param.18) | copy-start | bytes 4612
  78.9 21.7 %all-to-all-start.1 = ((bf16[64,8,384]{2,1,0:T(8,128)(2,1)}), bf16[64,8,384]{2,1,0:T(8,128)(2,1)S(1)}, u32[]{:S(2)}, u32[]{:S(2)}) async-start(bf16[64,8,384]{2,1,0:T(8,128)(2,1)} %bitcast.7), calls=%async_computation.1 | async-start | bytes 786432 | tf_op jit(solution)/shard_map/all_to_all | solution.py:261
  86.9 13.7 %copy-start.1 = (bf16[384,2048]{1,0:T(8,128)(2,1)S(1)}, bf16[384,2048]{1,0:T(8,128)(2,1)}, u32[]{:S(2)}) copy-start(bf16[384,2048]{1,0:T(8,128)(2,1)} %w_ref.1) | copy-start | bytes 4718596
  87.1 1.1 copy-start.8
  102.2 6.3 %collective-permute-start.11 = (bf16[512,256]{1,0:T(8,128)(2,1)S(1)}, bf16[512,256]{1,0:T(8,128)(2,1)S(1)}, u32[]{:S(2)}, u32[]{:S(2)}) collective-permute-start(bf16[512,256]{1,0:T(8,128)(2,1)S(1)} %get-tuple-element.68), channel_id=1, source_target_pairs={{0,1},{1,0},{2,3},{3,2},{4,5},{5,4},{6,7},{7,6},{8,9},{9,8},{10,11... | collective-permute-start | bytes 786440 | tf_op jit(solution)/shard_map/ppermute | solution.py:242
  104.2 12.6 %collective-permute-start.8 = (bf16[512,256]{1,0:T(8,128)(2,1)S(1)}, bf16[512,256]{1,0:T(8,128)(2,1)S(1)}, u32[]{:S(2)}, u32[]{:S(2)}) collective-permute-start(bf16[512,256]{1,0:T(8,128)(2,1)S(1)} %get-tuple-element.64), channel_id=1, source_target_pairs={{0,1},{1,0},{2,3},{3,2},{4,5},{5,4},{6,7},{7,6},{8,9},{9,8},{10,11... | collective-permute-start | bytes 786440 | tf_op jit(solution)/shard_map/ppermute | solution.py:242
  106.6 12.5 %collective-permute-start.10 = (bf16[512,256]{1,0:T(8,128)(2,1)S(1)}, bf16[512,256]{1,0:T(8,128)(2,1)S(1)}, u32[]{:S(2)}, u32[]{:S(2)}) collective-permute-start(bf16[512,256]{1,0:T(8,128)(2,1)S(1)} %get-tuple-element.66), channel_id=1, source_target_pairs={{0,1},{1,0},{2,3},{3,2},{4,5},{5,4},{6,7},{7,6},{8,9},{9,8},{10,11... | collective-permute-start | bytes 786440 | tf_op jit(solution)/shard_map/ppermute | solution.py:242
  108.5 29.4 %copy-start.9 = (f32[2,2,128,256]{3,2,1,0:T(8,128)S(1)}, f32[2,2,128,256]{3,2,1,0:T(8,128)}, u32[]{:S(2)}) copy-start(f32[2,2,128,256]{3,2,1,0:T(8,128)} %param.10) | copy-start | bytes 1572868
  108.6 10.5 %collective-permute-start.12 = (bf16[512,256]{1,0:T(8,128)(2,1)S(1)}, bf16[512,256]{1,0:T(8,128)(2,1)S(1)}, u32[]{:S(2)}, u32[]{:S(2)}) collective-permute-start(bf16[512,256]{1,0:T(8,128)(2,1)S(1)} %add_convert_fusion.1), channel_id=1, source_target_pairs={{0,2},{1,7},{2,4},{3,1},{4,6},{5,3},{6,0},{7,5},{8,10},{9,15},{10,... | collective-permute-start | bytes 786440 | tf_op jit(solution)/shard_map/ppermute | solution.py:238
  111.5 13.4 %collective-permute-start.7 = (bf16[512,256]{1,0:T(8,128)(2,1)S(1)}, bf16[512,256]{1,0:T(8,128)(2,1)S(1)}, u32[]{:S(2)}, u32[]{:S(2)}) collective-permute-start(bf16[512,256]{1,0:T(8,128)(2,1)S(1)} %get-tuple-element.62), channel_id=1, source_target_pairs={{0,1},{1,0},{2,3},{3,2},{4,5},{5,4},{6,7},{7,6},{8,9},{9,8},{10,11... | collective-permute-start | bytes 786440 | tf_op jit(solution)/shard_map/ppermute | solution.py:242
  116.8 16.3 %collective-permute-start.9 = (bf16[512,256]{1,0:T(8,128)(2,1)S(1)}, bf16[512,256]{1,0:T(8,128)(2,1)S(1)}, u32[]{:S(2)}, u32[]{:S(2)}) collective-permute-start(bf16[512,256]{1,0:T(8,128)(2,1)S(1)} %add_convert_fusion.2), channel_id=1, source_target_pairs={{0,6},{1,3},{2,0},{3,5},{4,2},{5,7},{6,4},{7,1},{8,14},{9,11},{10,... | collective-permute-start | bytes 786440 | tf_op jit(solution)/shard_map/ppermute | solution.py:238
  119.1 18.7 %collective-permute-start.13 = (bf16[512,256]{1,0:T(8,128)(2,1)S(1)}, bf16[512,256]{1,0:T(8,128)(2,1)S(1)}, u32[]{:S(2)}, u32[]{:S(2)}) collective-permute-start(bf16[512,256]{1,0:T(8,128)(2,1)S(1)} %add_convert_fusion), channel_id=1, source_target_pairs={{0,2},{1,7},{2,4},{3,1},{4,6},{5,3},{6,0},{7,5},{8,10},{9,15},{10,... | collective-permute-start | bytes 786440 | tf_op jit(solution)/shard_map/ppermute | solution.py:238
  (3 other events, 2.0 us)

commit v2 on v1

--- a/solution.py
+++ b/solution.py
@@ -38,12 +38,12 @@
 def spots():
     y_hi, core, way = position()
     other = 1 - core
-    early = [(y_hi, core), (y_hi - way, core), (y_hi + way, core)]
-    early += [(y_hi, other), (y_hi + way, other), (y_hi - way, other)]
-    return early, [(y_hi + 2, core), (y_hi + 2, other)]
-
-
-def scaled(pieces, gain_ref, squares, y_ref):
+    early = [(y_hi, core), (y_hi - way, core), (y_hi, other), (y_hi + way, other)]
+    late = [(y_hi + way, core), (y_hi + 2, core), (y_hi - way, other), (y_hi + 2, other)]
+    return early, late
+
+
+def scaled(pieces, gain_ref, squares, y_ref, counted=0):
     step_rows = 64
     part = pieces[0].shape[1]
     gains = [gain_ref[k : k + 1, :] for k in range(len(pieces))]
@@ -54,6 +54,8 @@
         for k, ref in enumerate(pieces):
             x = ref[rows, :].astype(F32)
             y_ref[rows, k * part : (k + 1) * part] = (x * gains[k]).astype(BF16)
+            if k < counted:
+                continue
             x = x * x
             for m in range(part // LANES):
                 total += x[:, m * LANES : (m + 1) * LANES]
@@ -99,28 +101,38 @@
         copy.wait()
 
 
+def squares_kernel(x_ref, squares_ref):
+    x = x_ref[...].astype(F32)
+    x = x * x
+    squares_ref[...] = x[:, :LANES] + x[:, LANES:]
+
+
 def first_kernel(*refs):
-    pieces = refs[:6]
-    w_ref, step_ref, gain_ref = refs[6:9]
-    acc_ref, squares_ref, y_ref = refs[9:]
+    pieces = refs[:4]
+    w_ref, step_ref, gain_ref, begun_ref = refs[4:8]
+    acc_ref, squares_ref, y_ref = refs[8:]
     wide = w_ref.shape[1]
-    scaled(pieces, gain_ref, lambda rows: jnp.zeros((64, LANES), F32), y_ref)(squares_ref)
+    scaled(pieces, gain_ref, lambda rows: begun_ref[rows, :], y_ref, 1)(squares_ref)
     y = y_ref[...]
     acc_ref[:, :wide] = dot(y, w_ref[...])
     acc_ref[:, wide:] = dot(y, step_ref[...], ((1,), (1,)))
 
 
+def gathered(x, b):
+    return jnp.concatenate([x[n * 128 + b * 64 : n * 128 + b * 64 + 64] for n in range(4)], axis=0)
+
+
 def project_kernel(*refs):
-    pieces = refs[:2]
-    w_ref, step_ref, gain_ref, small_ref, acc_ref, squares_ref = refs[2:8]
-    send_ref, inner_ref, value_ref, side_ref = refs[8:12]
-    y_ref, total_ref = refs[12:]
+    pieces = refs[:4]
+    w_ref, step_ref, gain_ref, small_ref, acc_ref, squares_ref = refs[4:10]
+    send_ref, inner_ref, value_ref, side_ref = refs[10:14]
+    y_ref, total_ref = refs[14:]
     patches = pieces[0].shape[0]
     channels = inner_ref.shape[1]
     wide = w_ref.shape[1]
     states = wide - channels
     scaled(pieces, gain_ref, lambda rows: squares_ref[rows, :], y_ref)(total_ref)
-    mean = jnp.sum(total_ref[...], axis=-1, keepdims=True) / (4 * y_ref.shape[1])
+    mean = jnp.sum(total_ref[...], axis=-1, keepdims=True) / (2 * y_ref.shape[1])
     scale = lax.rsqrt(mean + EPS)
     y = y_ref[...]
     raw = acc_ref[:, wide:] + dot(y, step_ref[...], ((1,), (1,)))
@@ -135,9 +147,12 @@
         widened = jnp.where(left, step[:, 2 * k : 2 * k + 1], step[:, 2 * k + 1 : 2 * k + 2])
         at = slice(k * LANES, (k + 1) * LANES)
         value_ref[:, at] = (inner[:, at].astype(F32) * widened).astype(BF16)
-    order = one_hot(patches, patches, lambda t: ((t & 3) << 7) + ((t >> 3) << 1) + ((t >> 2) & 1))
-    send_ref[:, :channels] = dot(order, value_ref[...]).astype(BF16)
-    send_ref[:, channels:] = dot(order, side_ref[...]).astype(BF16)
+    target = lambda t: ((t & 3) << 6) + ((t >> 3) << 1) + ((t >> 2) & 1)
+    order = one_hot(256, 256, target)
+    for b in range(patches // 256):
+        rows = slice(b * 256, (b + 1) * 256)
+        send_ref[rows, :channels] = dot(order, gathered(value_ref, b)).astype(BF16)
+        send_ref[rows, channels:] = dot(order, gathered(side_ref, b)).astype(BF16)
 
 
 def scan(value, side):
@@ -156,15 +171,22 @@
     shifted = running - decay.astype(F32)
     shifted_across = across - dot(decay, unit, ((0,), (0,)))
     doubled = jnp.where(t == r, 2.0 * scores, scores)
-    below = r <= t
-    outs = []
-    for h in range(heads):
+    below = r < t
+    left = lax.broadcasted_iota(jnp.int32, (length, LANES), 1) < HEAD_DIM
+
+    def weights(h):
         later = running[:, h : h + 1] - across[h : h + 1, :]
         earlier = shifted_across[h : h + 1, :] - shifted[:, h : h + 1]
-        weights = doubled * jnp.exp(jnp.where(below, jnp.where(t == r, 0.0, later), earlier))
-        outs.append(
-            dot(weights.astype(BF16), value[:, h * HEAD_DIM : (h + 1) * HEAD_DIM])
-        )
+        exponent = jnp.where(t == r, 0.0, jnp.where(below, later, earlier))
+        return (doubled * jnp.exp(exponent)).astype(BF16)
+
+    outs = []
+    for k in range(heads // 2):
+        pair = value[:, k * LANES : (k + 1) * LANES]
+        zero = jnp.zeros_like(pair)
+        stacked = jnp.concatenate([jnp.where(left, pair, zero), jnp.where(left, zero, pair)], axis=0)
+        both = jnp.concatenate([weights(2 * k), weights(2 * k + 1)], axis=1)
+        outs.append(dot(both, stacked))
     return jnp.concatenate(outs, axis=1)
 
 
@@ -182,31 +204,62 @@
     rows = recv_ref.shape[0]
     channels = back_ref.shape[1]
     length = rows // 4
-    order = one_hot(
-        rows, rows, lambda t: (((t & 127) >> 1) << 3) + ((t >> 7) << 1) + (t & 1)
-    )
-    sorted_ref[...] = dot(order, recv_ref[...]).astype(BF16)
+    order = one_hot(256, 256, lambda t: (((t & 63) >> 1) << 3) + ((t >> 6) << 1) + (t & 1))
+    for b in range(rows // 256):
+        block_rows = dot(order, recv_ref[b * 256 : (b + 1) * 256, :]).astype(BF16)
+        for n in range(4):
+            sorted_ref[n * length + b * 64 : n * length + b * 64 + 64, :] = block_rows[n * 64 : n * 64 + 64]
     for n in range(4):
         at = pl.ds(n * length, length)
         outs_ref[at, :] = scan(sorted_ref[at, :channels], sorted_ref[at, channels:]).astype(BF16)
-    back = one_hot(rows, rows, lambda t: (((t >> 1) & 3) << 7) + ((t >> 3) << 1) + (t & 1))
-    back_ref[...] = dot(back, outs_ref[...]).astype(BF16)
-
-
-def output_kernel(back_ref, row_ref, gain_ref, w_ref, *out_refs):
+    back = one_hot(256, 256, lambda t: (((t >> 1) & 3) << 6) + ((t >> 3) << 1) + (t & 1))
+    for b in range(rows // 256):
+        back_ref[b * 256 : (b + 1) * 256, :] = dot(back, gathered(outs_ref, b)).astype(BF16)
+
+
+def arrange_kernel(w_hbm, keep_ref, give_ref, sems):
     y_hi, core, way = position()
-    patches = row_ref.shape[0]
-    order = one_hot(
-        patches, patches, lambda t: (((t & 127) >> 1) << 3) + ((t & 1) << 2) + (t >> 7)
-    )
-    total = row_ref[...] + dot(order, back_ref[...])
-    scale = lax.rsqrt(jnp.mean(total * total, axis=-1, keepdims=True) + EPS)
-    gated = (total * scale * gain_ref[...]).astype(BF16)
-    part = out_refs[0].shape[1]
-    spots = [(2, 1 - core), (way, 1 - core), (-way, 1 - core), (0, 1 - core)]
-    spots += [(2, core), (-way, core), (way, core), (0, core)]
-    for ref, (chip, side) in zip(out_refs, spots):
-        ref[...] = dot(gated, w_ref[:, block(y_hi + chip, side, part)]).astype(ref.dtype)
+    part = keep_ref.shape[1] // 4
+    copies = []
+    for ref, side, toward in ((give_ref, 1 - core, -way), (keep_ref, core, way)):
+        for k, chip in enumerate((2, -toward, toward, 0)):
+            copy = pltpu.make_async_copy(
+                w_hbm.at[:, block(y_hi + chip, side, part)],
+                ref.at[:, pl.ds(k * part, part)],
+                sems.at[len(copies)],
+            )
+            copy.start()
+            copies.append(copy)
+    for copy in copies:
+        copy.wait()
+
+
+def gate_kernel(back_ref, row_ref, gain_ref, gated_ref):
+    order = one_hot(256, 256, lambda t: (((t & 63) >> 1) << 3) + ((t & 1) << 2) + (t >> 6))
+    for b in range(row_ref.shape[0] // 256):
+        total = gathered(row_ref, b) + dot(order, back_ref[b * 256 : (b + 1) * 256, :])
+        scale = lax.rsqrt(jnp.mean(total * total, axis=-1, keepdims=True) + EPS)
+        gated = (total * scale * gain_ref[...]).astype(BF16)
+        for n in range(4):
+            gated_ref[n * 128 + b * 64 : n * 128 + b * 64 + 64, :] = gated[n * 64 : n * 64 + 64]
+
+
+def far_kernel(gated_ref, peer_ref, keep_ref, got_ref, far_ref):
+    at = slice(0, far_ref.shape[1])
+    far_ref[...] = (
+        dot(gated_ref[...], keep_ref[:, at]) + dot(peer_ref[...], got_ref[:, at])
+    ).astype(BF16)
+
+
+def output_kernel(gated_ref, peer_ref, keep_ref, got_ref, tokens_ref, near_ref, last_ref, own_ref):
+    part = near_ref.shape[1]
+    gated, peer = gated_ref[...], peer_ref[...]
+    for k, ref in enumerate((near_ref, last_ref, own_ref)):
+        at = slice((k + 1) * part, (k + 2) * part)
+        total = dot(gated, keep_ref[:, at]) + dot(peer, got_ref[:, at])
+        if ref is own_ref:
+            total += tokens_ref[...]
+        ref[...] = total.astype(ref.dtype)
 
 
 def call(body, outs, args, flops, scratch=(), in_hbm=()):
@@ -264,32 +317,36 @@
     x = flat.astype(BF16)
     ahead, behind = hop(x, 1), hop(x, -1)
     wide = channels + 2 * STATE
-    counts = [6 * part, 2 * part]
+    counts = [4 * part, 4 * part]
     orders = [
         o
         for n in counts
         for o in (shape((n, wide), BF16), shape((LANES, n), BF16), shape((8, part), F32))
     ]
+    (begun,) = call(squares_kernel, [shape((patches, LANES), F32)], [x], 4 * 10**10)
+    begun, *sources = lax.optimization_barrier((begun, gain, w_inner, w_bc, w_step.T, bias, rate))
     prepared = call(
         prepare_kernel,
         orders + [shape((8, LANES), F32)],
-        [gain, w_inner, w_bc, w_step.T, bias, rate],
+        sources,
         4 * 10**9,
         [pltpu.SemaphoreType.DMA((16,))],
         in_hbm=(1, 2),
     )
     ahead, *prepared = lax.optimization_barrier((ahead, *prepared))
     across = hop(ahead, 1)
-    early = [x, ahead, behind, swap(x), swap(ahead), swap(behind)]
+    early = [x, ahead, swap(x), swap(ahead)]
     started = call(
         first_kernel,
         [shape((patches, wide + LANES), F32), shape((patches, LANES), F32)],
-        early + prepared[:3],
+        early + prepared[:3] + [begun],
         4 * 10**9,
         [pltpu.VMEM((patches, counts[0]), BF16)],
     )
-    across, *started = lax.optimization_barrier((across, *started))
-    pieces = [across, swap(across)]
+    behind, *started = lax.optimization_barrier((behind, *started))
+    peer_behind = swap(behind)
+    across, peer_behind = lax.optimization_barrier((across, peer_behind))
+    pieces = [behind, across, peer_behind, swap(across)]
     wide += LANES
     dims = [(patches, wide), (patches, channels), (patches, channels), (patches, wide - channels)]
     send, inner, value, side = call(
@@ -308,22 +365,33 @@
         [pltpu.VMEM((patches, wide), BF16), pltpu.VMEM((patches, channels), BF16)],
     )
     back = exchange(back)
+    w_keep, w_give = call(
+        arrange_kernel,
+        [shape((channels, 4 * part), BF16)] * 2,
+        [w_out],
+        10**7,
+        [pltpu.SemaphoreType.DMA((8,))],
+        in_hbm=(0,),
+    )
+    w_got = swap(w_give)
     (row,) = call(
         row_kernel, [shape((patches, channels), F32)], [value, side, inner, skip_wide], 8 * 10**8
     )
-    pieces = call(
+    (gated,) = call(
+        gate_kernel, [shape((patches, channels), BF16)], [back, row, out_gain], 4 * 10**8
+    )
+    operands = [gated, swap(gated), w_keep, w_got]
+    (far,) = call(far_kernel, [shape((patches, part), BF16)], operands, 4 * 10**8)
+    far = hop(far, 1)
+    near, next_sum, mine = call(
         output_kernel,
-        [shape((patches, part), BF16)] * 4 + [shape((patches, part), F32)] * 4,
-        [back, row, out_gain, w_out],
-        2 * patches * channels * 2048,
-    )
-    give, keep = pieces[:4], pieces[4:]
-    taken = [swap(g).astype(F32) for g in give]
-    sums = [k + t for k, t in zip(keep, taken)]
-    far = hop(sums[0].astype(BF16), 1)
-    near = hop(sums[1].astype(BF16), -1)
-    last = hop((sums[2] + far.astype(F32)).astype(BF16), 1)
-    total = flat + sums[3] + near.astype(F32) + last.astype(F32)
+        [shape((patches, part), BF16)] + [shape((patches, part), F32)] * 2,
+        operands + [flat],
+        2 * 10**9,
+    )
+    near = hop(near, -1)
+    last = hop((next_sum + far.astype(F32)).astype(BF16), 1)
+    total = mine + near.astype(F32) + last.astype(F32)
     return total.astype(BF16).reshape(tokens.shape)
 
 

time: 140 us -> 140 us (level)
  the two profiles are of different devices: /device:TPU:54 before, /device:TPU:104 now
where the time goes in v2:
time: 140 us; the launch traced here: 139 us
  blocking collectives  41.7 us (30%)
  waiting for transfers between devices  40.6 us (29%)
  starting transfers between devices  39.4 us (28%)
  Pallas kernels  12 us (9%)
  local copies, waits for them, and re-layouts  3.21 us (2%)
  other arithmetic  1.91 us (1%)
    all_to_all x1, blocking collectives, exchange(): y = lax.all_to_all(y, 'space', split_axis=0, concat_axis=0, tiled=True)  41.7 us
    ppermute x6, waiting for transfers between devices, hop(): return lax.ppermute(x, 'tensor', pairs)  31.6 us
    ppermute x6, starting transfers between devices, hop(): return lax.ppermute(x, 'tensor', pairs)  19.6 us
    pallas_call x10, Pallas kernels, call(): pl.pallas_call(body, out_shape=outs, in_specs=[pl.BlockSpec(memory_space=...  12 us
    ppermute x6, starting transfers between devices, swap(): return lax.ppermute(x, 'tensor', [(t, t ^ 1) for t in range(8)])  11.6 us
    all_to_all x1, starting transfers between devices, exchange(): y = lax.all_to_all(y, 'space', split_axis=0, concat_axis=0, tiled=True)  8.16 us
    all_to_all x1, waiting for transfers between devices, exchange(): y = lax.all_to_all(y, 'space', split_axis=0, concat_axis=0, tiled=True)  5.82 us
    ppermute x6, waiting for transfers between devices, swap(): return lax.ppermute(x, 'tensor', [(t, t ^ 1) for t in range(8)])  3.19 us
  transfers between devices with their start and end apart: 13, of which 8 were waited for; matrix products, arithmetic and copies ran while one was open for 0% of the time, Pallas kernels for 4%

profile of v2, /device:TPU:104, one launch (start us, length us, event | category | flops | bytes accessed | tf_op | source)
XLA Modules:
  0.0 139.2 jit_solution(10832892893221344752)
XLA Ops:
  1.1 3.0 %collective-permute-start.1 = (bf16[512,256]{1,0:T(8,128)(2,1)S(1)}, bf16[512,256]{1,0:T(8,128)(2,1)S(1)}, u32[]{:S(2)}, u32[]{:S(2)}) collective-permute-start(bf16[512,256]{1,0:T(8,128)(2,1)S(1)} %bitcast_convert_fusion.x_ref.refs_0_), channel_id=1, source_target_pairs={{0,2},{1,7},{2,4},{3,1},{4,6},{5,3},{6,0},{7,5},{8,10},{9,15},{10,... | collective-permute-start | bytes 786440 | tf_op jit(solution)/shard_map/ppermute | solution.py:291
  4.1 1.9 %collective-permute-start.2 = (bf16[512,256]{1,0:T(8,128)(2,1)S(1)}, bf16[512,256]{1,0:T(8,128)(2,1)S(1)}, u32[]{:S(2)}, u32[]{:S(2)}) collective-permute-start(bf16[512,256]{1,0:T(8,128)(2,1)S(1)} %bitcast_convert_fusion.x_ref.refs_0_), channel_id=1, source_target_pairs={{0,1},{1,0},{2,3},{3,2},{4,5},{5,4},{6,7},{7,6},{8,9},{9,8},{10,11... | collective-permute-start | bytes 786440 | tf_op jit(solution)/shard_map/ppermute | solution.py:295
  6.7 6.6 %collective-permute-done.1.refs_1_ = bf16[512,256]{1,0:T(8,128)(2,1)S(1)} collective-permute-done((bf16[512,256]{1,0:T(8,128)(2,1)S(1)}, bf16[512,256]{1,0:T(8,128)(2,1)S(1)}, u32[]{:S(2)}, u32[]{:S(2)}) %collective-permute-start.1) | collective-permute-done | bytes 262176 | tf_op jit(solution)/shard_map/ppermute | solution.py:291
  13.2 1.9 %collective-permute-start.3 = (bf16[512,256]{1,0:T(8,128)(2,1)S(1)}, bf16[512,256]{1,0:T(8,128)(2,1)S(1)}, u32[]{:S(2)}, u32[]{:S(2)}) collective-permute-start(bf16[512,256]{1,0:T(8,128)(2,1)S(1)} %collective-permute-done.1.refs_1_), channel_id=1, source_target_pairs={{0,1},{1,0},{2,3},{3,2},{4,5},{5,4},{6,7},{7,6},{8,9},{9,8},{10,11... | collective-permute-start | bytes 786440 | tf_op jit(solution)/shard_map/ppermute | solution.py:295
  15.2 3.2 %collective-permute-start = (bf16[512,256]{1,0:T(8,128)(2,1)S(1)}, bf16[512,256]{1,0:T(8,128)(2,1)S(1)}, u32[]{:S(2)}, u32[]{:S(2)}) collective-permute-start(bf16[512,256]{1,0:T(8,128)(2,1)S(1)} %bitcast_convert_fusion.x_ref.refs_0_), channel_id=1, source_target_pairs={{0,6},{1,3},{2,0},{3,5},{4,2},{5,7},{6,4},{7,1},{8,14},{9,11},{10,... | collective-permute-start | bytes 786440 | tf_op jit(solution)/shard_map/ppermute | solution.py:291
  18.3 3.6 %collective-permute-start.4 = (bf16[512,256]{1,0:T(8,128)(2,1)S(1)}, bf16[512,256]{1,0:T(8,128)(2,1)S(1)}, u32[]{:S(2)}, u32[]{:S(2)}) collective-permute-start(bf16[512,256]{1,0:T(8,128)(2,1)S(1)} %collective-permute-done.1.refs_1_), channel_id=1, source_target_pairs={{0,2},{1,7},{2,4},{3,1},{4,6},{5,3},{6,0},{7,5},{8,10},{9,15},{10,... | collective-permute-start | bytes 786440 | tf_op jit(solution)/shard_map/ppermute | solution.py:291
  23.5 3.0 %collective-permute-done.refs_0_ = bf16[512,256]{1,0:T(8,128)(2,1)S(1)} collective-permute-done((bf16[512,256]{1,0:T(8,128)(2,1)S(1)}, bf16[512,256]{1,0:T(8,128)(2,1)S(1)}, u32[]{:S(2)}, u32[]{:S(2)}) %collective-permute-start) | collective-permute-done | bytes 262176 | tf_op jit(solution)/shard_map/ppermute | solution.py:291
  26.5 1.9 %collective-permute-start.5 = (bf16[512,256]{1,0:T(8,128)(2,1)S(1)}, bf16[512,256]{1,0:T(8,128)(2,1)S(1)}, u32[]{:S(2)}, u32[]{:S(2)}) collective-permute-start(bf16[512,256]{1,0:T(8,128)(2,1)S(1)} %collective-permute-done.refs_0_), channel_id=1, source_target_pairs={{0,1},{1,0},{2,3},{3,2},{4,5},{5,4},{6,7},{7,6},{8,9},{9,8},{10,11... | collective-permute-start | bytes 786440 | tf_op jit(solution)/shard_map/ppermute | solution.py:295
  28.4 1.9 %collective-permute-done.4.refs_1_ = bf16[512,256]{1,0:T(8,128)(2,1)S(1)} collective-permute-done((bf16[512,256]{1,0:T(8,128)(2,1)S(1)}, bf16[512,256]{1,0:T(8,128)(2,1)S(1)}, u32[]{:S(2)}, u32[]{:S(2)}) %collective-permute-start.4) | collective-permute-done | bytes 262176 | tf_op jit(solution)/shard_map/ppermute | solution.py:291
  30.2 1.9 %collective-permute-start.6 = (bf16[512,256]{1,0:T(8,128)(2,1)S(1)}, bf16[512,256]{1,0:T(8,128)(2,1)S(1)}, u32[]{:S(2)}, u32[]{:S(2)}) collective-permute-start(bf16[512,256]{1,0:T(8,128)(2,1)S(1)} %collective-permute-done.4.refs_1_), channel_id=1, source_target_pairs={{0,1},{1,0},{2,3},{3,2},{4,5},{5,4},{6,7},{7,6},{8,9},{9,8},{10,11... | collective-permute-start | bytes 786440 | tf_op jit(solution)/shard_map/ppermute | solution.py:295
  33.7 2.2 %shard_map.103 = (bf16[512,768]{1,0:T(8,128)(2,1)S(1)}, bf16[512,384]{1,0:T(8,128)(2,1)S(1)}, bf16[512,384]{1,0:T(8,128)(2,1)S(1)}, bf16[512,384]{1,0:T(8,128)(2,1)S(1)}) custom-call(bf16[512,256]{1,0:T(8,128)(2,1)S(1)} %collective-permute-done.refs_0_, bf16[512,256]{1,0:T(8,128)(2,1)S(1)} %collective-permute-done.4.refs_1_, ...), custom_call_target="tpu_custom_call" | custom-call | flops 2000000000 | bytes 6434816 | tf_op jit(solution)/shard_map/pallas_call | solution.py:268
  35.8 41.7 %all_to_all.10 = bf16[64,8,768]{2,1,0:T(8,128)(2,1)S(1)} all-to-all(bf16[64,8,768]{2,1,0:T(8,128)(2,1)S(1)} %bitcast.12), channel_id=1, replica_groups=mesh['space'=64,'tensor'=8] {'space'}, dimensions={0} | all-to-all | bytes 1572864 | tf_op jit(solution)/shard_map/all_to_all | solution.py:314
  77.6 3.5 %shard_map.104 = bf16[512,384]{1,0:T(8,128)(2,1)} custom-call(bf16[512,768]{1,0:T(8,128)(2,1)S(1)} %bitcast.13), custom_call_target="tpu_custom_call" | custom-call | flops 800000000 | bytes 1179648 | tf_op jit(solution)/shard_map/pallas_call | solution.py:268
  81.1 8.2 %all-to-all-start.1 = ((bf16[64,8,384]{2,1,0:T(8,128)(2,1)}), bf16[64,8,384]{2,1,0:T(8,128)(2,1)S(1)}, u32[]{:S(2)}, u32[]{:S(2)}) async-start(bf16[64,8,384]{2,1,0:T(8,128)(2,1)} %bitcast.7), calls=%async_computation.1 | async-start | bytes 786432 | tf_op jit(solution)/shard_map/all_to_all | solution.py:314
  89.6 1.9 %collective-permute-start.8 = (bf16[384,1024]{1,0:T(8,128)(2,1)S(1)}, bf16[384,1024]{1,0:T(8,128)(2,1)S(1)}, u32[]{:S(2)}, u32[]{:S(2)}) collective-permute-start(bf16[384,1024]{1,0:T(8,128)(2,1)S(1)} %get-tuple-element.77), channel_id=1, source_target_pairs={{0,1},{1,0},{2,3},{3,2},{4,5},{5,4},{6,7},{7,6},{8,9},{9,8},{10,11... | collective-permute-start | bytes 2359304 | tf_op jit(solution)/shard_map/ppermute | solution.py:295
  94.7 2.1 %shard_map.105.row_ref = f32[512,384]{1,0:T(8,128)S(1)} custom-call(bf16[512,384]{1,0:T(8,128)(2,1)S(1)} %copy-done.11, bf16[512,384]{1,0:T(8,128)(2,1)S(1)} %copy-done.13, bf16[512,384]{1,0:T(8,128)(2,1)S(1)} %copy-done.9, f32[1,384]{1,0:T(1,128)S(1)} %broadcast_in_dim_reshape.3.skip_ref), custom_call_target="tpu_custom_call" | custom-call | flops 800000000 | bytes 1967616 | tf_op jit(solution)/shard_map/pallas_call | solution.py:268
  96.8 5.8 %all-to-all-done.1 = bf16[64,8,384]{2,1,0:T(8,128)(2,1)S(1)} async-done(((bf16[64,8,384]{2,1,0:T(8,128)(2,1)}), bf16[64,8,384]{2,1,0:T(8,128)(2,1)S(1)}, u32[]{:S(2)}, u32[]{:S(2)}) %all-to-all-start.1) | async-done | bytes 393248 | tf_op jit(solution)/shard_map/all_to_all | solution.py:314
  103.0 2.1 %collective-permute-start.7 = (bf16[512,384]{1,0:T(8,128)(2,1)S(1)}, bf16[512,384]{1,0:T(8,128)(2,1)S(1)}, u32[]{:S(2)}, u32[]{:S(2)}) collective-permute-start(bf16[512,384]{1,0:T(8,128)(2,1)S(1)} %shard_map.106.gated_ref), channel_id=1, source_target_pairs={{0,1},{1,0},{2,3},{3,2},{4,5},{5,4},{6,7},{7,6},{8,9},{9,8},{10,11... | collective-permute-start | bytes 1179656 | tf_op jit(solution)/shard_map/ppermute | solution.py:295
  105.1 1.7 %collective-permute-done.7.peer_ref = bf16[512,384]{1,0:T(8,128)(2,1)S(1)} collective-permute-done((bf16[512,384]{1,0:T(8,128)(2,1)S(1)}, bf16[512,384]{1,0:T(8,128)(2,1)S(1)}, u32[]{:S(2)}, u32[]{:S(2)}) %collective-permute-start.7) | collective-permute-done | bytes 393248 | tf_op jit(solution)/shard_map/ppermute | solution.py:295
  107.2 2.5 %collective-permute-start.10 = (bf16[512,256]{1,0:T(8,128)(2,1)S(1)}, bf16[512,256]{1,0:T(8,128)(2,1)S(1)}, u32[]{:S(2)}, u32[]{:S(2)}) collective-permute-start(bf16[512,256]{1,0:T(8,128)(2,1)S(1)} %shard_map.109), channel_id=1, source_target_pairs={{0,2},{1,7},{2,4},{3,1},{4,6},{5,3},{6,0},{7,5},{8,10},{9,15},{10,... | collective-permute-start | bytes 786440 | tf_op jit(solution)/shard_map/ppermute | solution.py:291
  110.7 5.4 %collective-permute-start.9 = (bf16[512,256]{1,0:T(8,128)(2,1)S(1)}, bf16[512,256]{1,0:T(8,128)(2,1)S(1)}, u32[]{:S(2)}, u32[]{:S(2)}) collective-permute-start(bf16[512,256]{1,0:T(8,128)(2,1)S(1)} %get-tuple-element.79), channel_id=1, source_target_pairs={{0,6},{1,3},{2,0},{3,5},{4,2},{5,7},{6,4},{7,1},{8,14},{9,11},{10,... | collective-permute-start | bytes 786440 | tf_op jit(solution)/shard_map/ppermute | solution.py:291
  116.2 9.1 %collective-permute-done.10 = bf16[512,256]{1,0:T(8,128)(2,1)S(1)} collective-permute-done((bf16[512,256]{1,0:T(8,128)(2,1)S(1)}, bf16[512,256]{1,0:T(8,128)(2,1)S(1)}, u32[]{:S(2)}, u32[]{:S(2)}) %collective-permute-start.10) | collective-permute-done | bytes 262176 | tf_op jit(solution)/shard_map/ppermute | solution.py:291
  125.3 1.9 %collective-permute-start.11 = (bf16[512,256]{1,0:T(8,128)(2,1)S(1)}, bf16[512,256]{1,0:T(8,128)(2,1)S(1)}, u32[]{:S(2)}, u32[]{:S(2)}) collective-permute-start(bf16[512,256]{1,0:T(8,128)(2,1)S(1)} %add_convert_fusion.1), channel_id=1, source_target_pairs={{0,2},{1,7},{2,4},{3,1},{4,6},{5,3},{6,0},{7,5},{8,10},{9,15},{10,... | collective-permute-start | bytes 786440 | tf_op jit(solution)/shard_map/ppermute | solution.py:291
  127.3 11.1 %collective-permute-done.11 = bf16[512,256]{1,0:T(8,128)(2,1)S(1)} collective-permute-done((bf16[512,256]{1,0:T(8,128)(2,1)S(1)}, bf16[512,256]{1,0:T(8,128)(2,1)S(1)}, u32[]{:S(2)}, u32[]{:S(2)}) %collective-permute-start.11) | collective-permute-done | bytes 262176 | tf_op jit(solution)/shard_map/ppermute | solution.py:291
  (51 shorter events, 10.9 us)
Async XLA Ops:
  1.1 5.0 %copy-start.2 = (bf16[2048,384]{1,0:T(8,128)(2,1)S(1)}, bf16[2048,384]{1,0:T(8,128)(2,1)}, u32[]{:S(2)}) copy-start(bf16[2048,384]{1,0:T(8,128)(2,1)} %refs_1_) | copy-start | bytes 4718596
  1.1 5.0 %copy-start.3 = (bf16[2048,256]{1,0:T(8,128)(2,1)S(1)}, bf16[2048,256]{1,0:T(8,128)(2,1)}, u32[]{:S(2)}) copy-start(bf16[2048,256]{1,0:T(8,128)(2,1)} %refs_2_) | copy-start | bytes 3145732
  1.1 5.0 %copy-start.4 = (bf16[2048,6]{0,1:T(8,128)(2,1)S(1)}, bf16[2048,6]{0,1:T(8,128)(2,1)}, u32[]{:S(2)}) copy-start(bf16[2048,6]{0,1:T(8,128)(2,1)} %param.14) | copy-start | bytes 73732
  1.1 5.0 %copy-start.5 = (f32[2048]{0:T(1024)S(1)}, f32[2048]{0:T(1024)}, u32[]{:S(2)}) copy-start(f32[2048]{0:T(1024)} %param.11) | copy-start | bytes 24580
  1.1 12.1 %collective-permute-start.1 = (bf16[512,256]{1,0:T(8,128)(2,1)S(1)}, bf16[512,256]{1,0:T(8,128)(2,1)S(1)}, u32[]{:S(2)}, u32[]{:S(2)}) collective-permute-start(bf16[512,256]{1,0:T(8,128)(2,1)S(1)} %bitcast_convert_fusion.x_ref.refs_0_), channel_id=1, source_target_pairs={{0,2},{1,7},{2,4},{3,1},{4,6},{5,3},{6,0},{7,5},{8,10},{9,15},{10,... | collective-permute-start | bytes 786440 | tf_op jit(solution)/shard_map/ppermute | solution.py:291
  4.1 17.8 %collective-permute-start.2 = (bf16[512,256]{1,0:T(8,128)(2,1)S(1)}, bf16[512,256]{1,0:T(8,128)(2,1)S(1)}, u32[]{:S(2)}, u32[]{:S(2)}) collective-permute-start(bf16[512,256]{1,0:T(8,128)(2,1)S(1)} %bitcast_convert_fusion.x_ref.refs_0_), channel_id=1, source_target_pairs={{0,1},{1,0},{2,3},{3,2},{4,5},{5,4},{6,7},{7,6},{8,9},{9,8},{10,11... | collective-permute-start | bytes 786440 | tf_op jit(solution)/shard_map/ppermute | solution.py:295
  13.2 8.7 %collective-permute-start.3 = (bf16[512,256]{1,0:T(8,128)(2,1)S(1)}, bf16[512,256]{1,0:T(8,128)(2,1)S(1)}, u32[]{:S(2)}, u32[]{:S(2)}) collective-permute-start(bf16[512,256]{1,0:T(8,128)(2,1)S(1)} %collective-permute-done.1.refs_1_), channel_id=1, source_target_pairs={{0,1},{1,0},{2,3},{3,2},{4,5},{5,4},{6,7},{7,6},{8,9},{9,8},{10,11... | collective-permute-start | bytes 786440 | tf_op jit(solution)/shard_map/ppermute | solution.py:295
  15.2 11.3 %collective-permute-start = (bf16[512,256]{1,0:T(8,128)(2,1)S(1)}, bf16[512,256]{1,0:T(8,128)(2,1)S(1)}, u32[]{:S(2)}, u32[]{:S(2)}) collective-permute-start(bf16[512,256]{1,0:T(8,128)(2,1)S(1)} %bitcast_convert_fusion.x_ref.refs_0_), channel_id=1, source_target_pairs={{0,6},{1,3},{2,0},{3,5},{4,2},{5,7},{6,4},{7,1},{8,14},{9,11},{10,... | collective-permute-start | bytes 786440 | tf_op jit(solution)/shard_map/ppermute | solution.py:291
  18.3 11.9 %collective-permute-start.4 = (bf16[512,256]{1,0:T(8,128)(2,1)S(1)}, bf16[512,256]{1,0:T(8,128)(2,1)S(1)}, u32[]{:S(2)}, u32[]{:S(2)}) collective-permute-start(bf16[512,256]{1,0:T(8,128)(2,1)S(1)} %collective-permute-done.1.refs_1_), channel_id=1, source_target_pairs={{0,2},{1,7},{2,4},{3,1},{4,6},{5,3},{6,0},{7,5},{8,10},{9,15},{10,... | collective-permute-start | bytes 786440 | tf_op jit(solution)/shard_map/ppermute | solution.py:291
  26.5 3.8 %collective-permute-start.5 = (bf16[512,256]{1,0:T(8,128)(2,1)S(1)}, bf16[512,256]{1,0:T(8,128)(2,1)S(1)}, u32[]{:S(2)}, u32[]{:S(2)}) collective-permute-start(bf16[512,256]{1,0:T(8,128)(2,1)S(1)} %collective-permute-done.refs_0_), channel_id=1, source_target_pairs={{0,1},{1,0},{2,3},{3,2},{4,5},{5,4},{6,7},{7,6},{8,9},{9,8},{10,11... | collective-permute-start | bytes 786440 | tf_op jit(solution)/shard_map/ppermute | solution.py:295
  30.2 3.4 %collective-permute-start.6 = (bf16[512,256]{1,0:T(8,128)(2,1)S(1)}, bf16[512,256]{1,0:T(8,128)(2,1)S(1)}, u32[]{:S(2)}, u32[]{:S(2)}) collective-permute-start(bf16[512,256]{1,0:T(8,128)(2,1)S(1)} %collective-permute-done.4.refs_1_), channel_id=1, source_target_pairs={{0,1},{1,0},{2,3},{3,2},{4,5},{5,4},{6,7},{7,6},{8,9},{9,8},{10,11... | collective-permute-start | bytes 786440 | tf_op jit(solution)/shard_map/ppermute | solution.py:295
  35.8 45.2 %copy-start.8 = (bf16[512,384]{1,0:T(8,128)(2,1)}, bf16[512,384]{1,0:T(8,128)(2,1)S(1)}, u32[]{:S(2)}) copy-start(bf16[512,384]{1,0:T(8,128)(2,1)S(1)} %get-tuple-element.75.inner_ref) | copy-start | bytes 1179652
  35.8 45.2 %copy-start.10 = (bf16[512,384]{1,0:T(8,128)(2,1)}, bf16[512,384]{1,0:T(8,128)(2,1)S(1)}, u32[]{:S(2)}) copy-start(bf16[512,384]{1,0:T(8,128)(2,1)S(1)} %get-tuple-element.73.value_ref) | copy-start | bytes 1179652
  35.8 45.2 %copy-start.12 = (bf16[512,384]{1,0:T(8,128)(2,1)}, bf16[512,384]{1,0:T(8,128)(2,1)S(1)}, u32[]{:S(2)}) copy-start(bf16[512,384]{1,0:T(8,128)(2,1)S(1)} %get-tuple-element.74.side_ref) | copy-start | bytes 1179652
  77.6 11.7 %copy-start = (bf16[384,2048]{1,0:T(8,128)(2,1)S(1)}, bf16[384,2048]{1,0:T(8,128)(2,1)}, u32[]{:S(2)}) copy-start(bf16[384,2048]{1,0:T(8,128)(2,1)} %w_hbm.1) | copy-start | bytes 4718596
  81.0 10.5 %copy-start.15 = (f32[6]{0:T(128)S(1)}, f32[6]{0:T(128)}, u32[]{:S(2)}) copy-start(f32[6]{0:T(128)} %param.17) | copy-start | bytes 76
  81.0 10.6 %copy-start.14 = (f32[384]{0:T(512)S(1)}, f32[384]{0:T(512)}, u32[]{:S(2)}) copy-start(f32[384]{0:T(512)} %param.18) | copy-start | bytes 4612
  81.1 21.6 %all-to-all-start.1 = ((bf16[64,8,384]{2,1,0:T(8,128)(2,1)}), bf16[64,8,384]{2,1,0:T(8,128)(2,1)S(1)}, u32[]{:S(2)}, u32[]{:S(2)}) async-start(bf16[64,8,384]{2,1,0:T(8,128)(2,1)} %bitcast.7), calls=%async_computation.1 | async-start | bytes 786432 | tf_op jit(solution)/shard_map/all_to_all | solution.py:314
  89.6 15.5 %collective-permute-start.8 = (bf16[384,1024]{1,0:T(8,128)(2,1)S(1)}, bf16[384,1024]{1,0:T(8,128)(2,1)S(1)}, u32[]{:S(2)}, u32[]{:S(2)}) collective-permute-start(bf16[384,1024]{1,0:T(8,128)(2,1)S(1)} %get-tuple-element.77), channel_id=1, source_target_pairs={{0,1},{1,0},{2,3},{3,2},{4,5},{5,4},{6,7},{7,6},{8,9},{9,8},{10,11... | collective-permute-start | bytes 2359304 | tf_op jit(solution)/shard_map/ppermute | solution.py:295
  103.0 6.7 %copy-start.1 = (f32[2,2,128,256]{3,2,1,0:T(8,128)S(1)}, f32[2,2,128,256]{3,2,1,0:T(8,128)}, u32[]{:S(2)}) copy-start(f32[2,2,128,256]{3,2,1,0:T(8,128)} %param.10) | copy-start | bytes 1572868
  103.0 3.7 %collective-permute-start.7 = (bf16[512,384]{1,0:T(8,128)(2,1)S(1)}, bf16[512,384]{1,0:T(8,128)(2,1)S(1)}, u32[]{:S(2)}, u32[]{:S(2)}) collective-permute-start(bf16[512,384]{1,0:T(8,128)(2,1)S(1)} %shard_map.106.gated_ref), channel_id=1, source_target_pairs={{0,1},{1,0},{2,3},{3,2},{4,5},{5,4},{6,7},{7,6},{8,9},{9,8},{10,11... | collective-permute-start | bytes 1179656 | tf_op jit(solution)/shard_map/ppermute | solution.py:295
  107.2 18.0 %collective-permute-start.10 = (bf16[512,256]{1,0:T(8,128)(2,1)S(1)}, bf16[512,256]{1,0:T(8,128)(2,1)S(1)}, u32[]{:S(2)}, u32[]{:S(2)}) collective-permute-start(bf16[512,256]{1,0:T(8,128)(2,1)S(1)} %shard_map.109), channel_id=1, source_target_pairs={{0,2},{1,7},{2,4},{3,1},{4,6},{5,3},{6,0},{7,5},{8,10},{9,15},{10,... | collective-permute-start | bytes 786440 | tf_op jit(solution)/shard_map/ppermute | solution.py:291
  110.7 16.5 %collective-permute-start.9 = (bf16[512,256]{1,0:T(8,128)(2,1)S(1)}, bf16[512,256]{1,0:T(8,128)(2,1)S(1)}, u32[]{:S(2)}, u32[]{:S(2)}) collective-permute-start(bf16[512,256]{1,0:T(8,128)(2,1)S(1)} %get-tuple-element.79), channel_id=1, source_target_pairs={{0,6},{1,3},{2,0},{3,5},{4,2},{5,7},{6,4},{7,1},{8,14},{9,11},{10,... | collective-permute-start | bytes 786440 | tf_op jit(solution)/shard_map/ppermute | solution.py:291
  125.3 13.1 %collective-permute-start.11 = (bf16[512,256]{1,0:T(8,128)(2,1)S(1)}, bf16[512,256]{1,0:T(8,128)(2,1)S(1)}, u32[]{:S(2)}, u32[]{:S(2)}) collective-permute-start(bf16[512,256]{1,0:T(8,128)(2,1)S(1)} %add_convert_fusion.1), channel_id=1, source_target_pairs={{0,2},{1,7},{2,4},{3,1},{4,6},{5,3},{6,0},{7,5},{8,10},{9,15},{10,... | collective-permute-start | bytes 786440 | tf_op jit(solution)/shard_map/ppermute | solution.py:291
  (5 other events, 13.0 us)

commit v3 on v2

--- a/solution.py
+++ b/solution.py
@@ -177,8 +177,7 @@
     def weights(h):
         later = running[:, h : h + 1] - across[h : h + 1, :]
         earlier = shifted_across[h : h + 1, :] - shifted[:, h : h + 1]
-        exponent = jnp.where(t == r, 0.0, jnp.where(below, later, earlier))
-        return (doubled * jnp.exp(exponent)).astype(BF16)
+        return (doubled * jnp.exp(jnp.where(below, later, earlier))).astype(BF16)
 
     outs = []
     for k in range(heads // 2):
@@ -192,11 +191,19 @@
 
 def row_kernel(value_ref, side_ref, inner_ref, skip_ref, out_ref):
     length = LANES
+    left = lax.broadcasted_iota(jnp.int32, (1, LANES), 1) < HEAD_DIM
+    heads = skip_ref.shape[1]
+    skip = jnp.concatenate(
+        [
+            jnp.where(left, skip_ref[0:1, k : k + 1], skip_ref[0:1, k + 1 : k + 2])
+            for k in range(0, heads, 2)
+        ],
+        axis=1,
+    )
     for row in range(value_ref.shape[0] // length):
         at = pl.ds(row * length, length)
         out_ref[at, :] = (
-            scan(value_ref[at, :], side_ref[at, :])
-            + skip_ref[...] * inner_ref[at, :].astype(F32)
+            scan(value_ref[at, :], side_ref[at, :]) + skip * inner_ref[at, :].astype(F32)
         )
 
 
@@ -236,10 +243,11 @@
 
 def gate_kernel(back_ref, row_ref, gain_ref, gated_ref):
     order = one_hot(256, 256, lambda t: (((t & 63) >> 1) << 3) + ((t & 1) << 2) + (t >> 6))
+    gain = jnp.concatenate([gain_ref[k : k + 1, :] for k in range(gain_ref.shape[0])], axis=1)
     for b in range(row_ref.shape[0] // 256):
         total = gathered(row_ref, b) + dot(order, back_ref[b * 256 : (b + 1) * 256, :])
         scale = lax.rsqrt(jnp.mean(total * total, axis=-1, keepdims=True) + EPS)
-        gated = (total * scale * gain_ref[...]).astype(BF16)
+        gated = (total * scale * gain).astype(BF16)
         for n in range(4):
             gated_ref[n * 128 + b * 64 : n * 128 + b * 64 + 64, :] = gated[n * 64 : n * 64 + 64]
 
@@ -304,8 +312,7 @@
     gain = in_gain.reshape(-1, LANES)
     bias = step_bias[None, :]
     rate = decay_rate[None, :]
-    skip_wide = jnp.repeat(skip, HEAD_DIM)[None, :]
-    out_gain = norm_gain[None, :]
+    out_gain = norm_gain.reshape(-1, LANES)
     flat = tokens.reshape(patches, part)
     space = lax.axis_size("space")
 
@@ -343,9 +350,8 @@
         4 * 10**9,
         [pltpu.VMEM((patches, counts[0]), BF16)],
     )
-    behind, *started = lax.optimization_barrier((behind, *started))
     peer_behind = swap(behind)
-    across, peer_behind = lax.optimization_barrier((across, peer_behind))
+    across, peer_behind, *started = lax.optimization_barrier((across, peer_behind, *started))
     pieces = [behind, across, peer_behind, swap(across)]
     wide += LANES
     dims = [(patches, wide), (patches, channels), (patches, channels), (patches, wide - channels)]
@@ -375,7 +381,7 @@
     )
     w_got = swap(w_give)
     (row,) = call(
-        row_kernel, [shape((patches, channels), F32)], [value, side, inner, skip_wide], 8 * 10**8
+        row_kernel, [shape((patches, channels), F32)], [value, side, inner, skip[None, :]], 8 * 10**8
     )
     (gated,) = call(
         gate_kernel, [shape((patches, channels), BF16)], [back, row, out_gain], 4 * 10**8

time: 140 us -> 132 us (0.943)
  the two profiles are of different devices: /device:TPU:104 before, /device:TPU:40 now
where the time goes in v3:
time: 132 us
  waiting for transfers between devices  41.7 us (32%)
  starting transfers between devices  39.9 us (30%)
  blocking collectives  36 us (27%)
  Pallas kernels  12 us (9%)
  other arithmetic  1.91 us (1%)
    all_to_all x1, blocking collectives, exchange(): y = lax.all_to_all(y, 'space', split_axis=0, concat_axis=0, tiled=True)  36 us
    ppermute x6, waiting for transfers between devices, hop(): return lax.ppermute(x, 'tensor', pairs)  28.4 us
    ppermute x6, starting transfers between devices, hop(): return lax.ppermute(x, 'tensor', pairs)  20 us
    ppermute x6, starting transfers between devices, swap(): return lax.ppermute(x, 'tensor', [(t, t ^ 1) for t in range(8)])  12.1 us
    pallas_call x10, Pallas kernels, call(): pl.pallas_call(body, out_shape=outs, in_specs=[pl.BlockSpec(memory_space=...  12 us
    all_to_all x1, waiting for transfers between devices, exchange(): y = lax.all_to_all(y, 'space', split_axis=0, concat_axis=0, tiled=True)  10 us
    all_to_all x1, starting transfers between devices, exchange(): y = lax.all_to_all(y, 'space', split_axis=0, concat_axis=0, tiled=True)  7.75 us
    ppermute x6, waiting for transfers between devices, swap(): return lax.ppermute(x, 'tensor', [(t, t ^ 1) for t in range(8)])  3.19 us
  transfers between devices with their start and end apart: 13, of which 7 were waited for; matrix products, arithmetic and copies ran while one was open for 0% of the time, Pallas kernels for 5%

profile of v3, /device:TPU:40, one launch (start us, length us, event | category | flops | bytes accessed | tf_op | source)
XLA Modules:
  0.0 131.9 jit_solution(14570768487445890279)
XLA Ops:
  1.1 3.0 %collective-permute-start.1 = (bf16[512,256]{1,0:T(8,128)(2,1)S(1)}, bf16[512,256]{1,0:T(8,128)(2,1)S(1)}, u32[]{:S(2)}, u32[]{:S(2)}) collective-permute-start(bf16[512,256]{1,0:T(8,128)(2,1)S(1)} %bitcast_convert_fusion.x_ref.refs_0_), channel_id=1, source_target_pairs={{0,2},{1,7},{2,4},{3,1},{4,6},{5,3},{6,0},{7,5},{8,10},{9,15},{10,... | collective-permute-start | bytes 786440 | tf_op jit(solution)/shard_map/ppermute | solution.py:299
  4.1 1.9 %collective-permute-start.4 = (bf16[512,256]{1,0:T(8,128)(2,1)S(1)}, bf16[512,256]{1,0:T(8,128)(2,1)S(1)}, u32[]{:S(2)}, u32[]{:S(2)}) collective-permute-start(bf16[512,256]{1,0:T(8,128)(2,1)S(1)} %bitcast_convert_fusion.x_ref.refs_0_), channel_id=1, source_target_pairs={{0,1},{1,0},{2,3},{3,2},{4,5},{5,4},{6,7},{7,6},{8,9},{9,8},{10,11... | collective-permute-start | bytes 786440 | tf_op jit(solution)/shard_map/ppermute | solution.py:303
  6.0 5.3 %collective-permute-start = (bf16[512,256]{1,0:T(8,128)(2,1)S(1)}, bf16[512,256]{1,0:T(8,128)(2,1)S(1)}, u32[]{:S(2)}, u32[]{:S(2)}) collective-permute-start(bf16[512,256]{1,0:T(8,128)(2,1)S(1)} %bitcast_convert_fusion.x_ref.refs_0_), channel_id=1, source_target_pairs={{0,6},{1,3},{2,0},{3,5},{4,2},{5,7},{6,4},{7,1},{8,14},{9,11},{10,... | collective-permute-start | bytes 786440 | tf_op jit(solution)/shard_map/ppermute | solution.py:299
  11.9 4.2 %collective-permute-done.1.refs_1_ = bf16[512,256]{1,0:T(8,128)(2,1)S(1)} collective-permute-done((bf16[512,256]{1,0:T(8,128)(2,1)S(1)}, bf16[512,256]{1,0:T(8,128)(2,1)S(1)}, u32[]{:S(2)}, u32[]{:S(2)}) %collective-permute-start.1) | collective-permute-done | bytes 262176 | tf_op jit(solution)/shard_map/ppermute | solution.py:299
  16.1 1.9 %collective-permute-start.5 = (bf16[512,256]{1,0:T(8,128)(2,1)S(1)}, bf16[512,256]{1,0:T(8,128)(2,1)S(1)}, u32[]{:S(2)}, u32[]{:S(2)}) collective-permute-start(bf16[512,256]{1,0:T(8,128)(2,1)S(1)} %collective-permute-done.1.refs_1_), channel_id=1, source_target_pairs={{0,1},{1,0},{2,3},{3,2},{4,5},{5,4},{6,7},{7,6},{8,9},{9,8},{10,11... | collective-permute-start | bytes 786440 | tf_op jit(solution)/shard_map/ppermute | solution.py:303
  18.0 1.9 %collective-permute-start.2 = (bf16[512,256]{1,0:T(8,128)(2,1)S(1)}, bf16[512,256]{1,0:T(8,128)(2,1)S(1)}, u32[]{:S(2)}, u32[]{:S(2)}) collective-permute-start(bf16[512,256]{1,0:T(8,128)(2,1)S(1)} %collective-permute-done.1.refs_1_), channel_id=1, source_target_pairs={{0,2},{1,7},{2,4},{3,1},{4,6},{5,3},{6,0},{7,5},{8,10},{9,15},{10,... | collective-permute-start | bytes 786440 | tf_op jit(solution)/shard_map/ppermute | solution.py:299
  20.0 2.4 %collective-permute-start.3 = (bf16[512,256]{1,0:T(8,128)(2,1)S(1)}, bf16[512,256]{1,0:T(8,128)(2,1)S(1)}, u32[]{:S(2)}, u32[]{:S(2)}) collective-permute-start(bf16[512,256]{1,0:T(8,128)(2,1)S(1)} %collective-permute-done.refs_0_), channel_id=1, source_target_pairs={{0,1},{1,0},{2,3},{3,2},{4,5},{5,4},{6,7},{7,6},{8,9},{9,8},{10,11... | collective-permute-start | bytes 786440 | tf_op jit(solution)/shard_map/ppermute | solution.py:303
  22.4 1.6 %shard_map.102 = (f32[512,768]{1,0:T(8,128)S(1)}, f32[512,128]{1,0:T(8,128)S(1)}) custom-call(bf16[512,256]{1,0:T(8,128)(2,1)S(1)} %bitcast_convert_fusion.x_ref.refs_0_, bf16[512,256]{1,0:T(8,128)(2,1)S(1)} %collective-permute-done.1.refs_1_, bf16[512,256]{1,0:T(8,128)(2,1)S(1)} %collective-permute-done.4.refs_2_, ...), custom_call_target="tpu_custom_call" | custom-call | flops 4000000000 | bytes 4726784 | tf_op jit(solution)/shard_map/pallas_call | solution.py:276
  24.0 7.2 %collective-permute-done.2.refs_1_ = bf16[512,256]{1,0:T(8,128)(2,1)S(1)} collective-permute-done((bf16[512,256]{1,0:T(8,128)(2,1)S(1)}, bf16[512,256]{1,0:T(8,128)(2,1)S(1)}, u32[]{:S(2)}, u32[]{:S(2)}) %collective-permute-start.2) | collective-permute-done | bytes 262176 | tf_op jit(solution)/shard_map/ppermute | solution.py:299
  31.2 1.9 %collective-permute-start.6 = (bf16[512,256]{1,0:T(8,128)(2,1)S(1)}, bf16[512,256]{1,0:T(8,128)(2,1)S(1)}, u32[]{:S(2)}, u32[]{:S(2)}) collective-permute-start(bf16[512,256]{1,0:T(8,128)(2,1)S(1)} %collective-permute-done.2.refs_1_), channel_id=1, source_target_pairs={{0,1},{1,0},{2,3},{3,2},{4,5},{5,4},{6,7},{7,6},{8,9},{9,8},{10,11... | collective-permute-start | bytes 786440 | tf_op jit(solution)/shard_map/ppermute | solution.py:303
  34.6 2.1 %shard_map.103 = (bf16[512,768]{1,0:T(8,128)(2,1)S(1)}, bf16[512,384]{1,0:T(8,128)(2,1)S(1)}, bf16[512,384]{1,0:T(8,128)(2,1)S(1)}, bf16[512,384]{1,0:T(8,128)(2,1)S(1)}) custom-call(bf16[512,256]{1,0:T(8,128)(2,1)S(1)} %collective-permute-done.refs_0_, bf16[512,256]{1,0:T(8,128)(2,1)S(1)} %collective-permute-done.2.refs_1_, ...), custom_call_target="tpu_custom_call" | custom-call | flops 2000000000 | bytes 6434816 | tf_op jit(solution)/shard_map/pallas_call | solution.py:276
  36.8 36.0 %all_to_all.10 = bf16[64,8,768]{2,1,0:T(8,128)(2,1)S(1)} all-to-all(bf16[64,8,768]{2,1,0:T(8,128)(2,1)S(1)} %bitcast.14), channel_id=1, replica_groups=mesh['space'=64,'tensor'=8] {'space'}, dimensions={0} | all-to-all | bytes 1572864 | tf_op jit(solution)/shard_map/all_to_all | solution.py:321
  72.8 3.5 %shard_map.104 = bf16[512,384]{1,0:T(8,128)(2,1)} custom-call(bf16[512,768]{1,0:T(8,128)(2,1)S(1)} %bitcast.15), custom_call_target="tpu_custom_call" | custom-call | flops 800000000 | bytes 1179648 | tf_op jit(solution)/shard_map/pallas_call | solution.py:276
  76.3 7.7 %all-to-all-start.1 = ((bf16[64,8,384]{2,1,0:T(8,128)(2,1)}), bf16[64,8,384]{2,1,0:T(8,128)(2,1)S(1)}, u32[]{:S(2)}, u32[]{:S(2)}) async-start(bf16[64,8,384]{2,1,0:T(8,128)(2,1)} %bitcast.7), calls=%async_computation.1 | async-start | bytes 786432 | tf_op jit(solution)/shard_map/all_to_all | solution.py:321
  84.4 1.9 %collective-permute-start.8 = (bf16[384,1024]{1,0:T(8,128)(2,1)S(1)}, bf16[384,1024]{1,0:T(8,128)(2,1)S(1)}, u32[]{:S(2)}, u32[]{:S(2)}) collective-permute-start(bf16[384,1024]{1,0:T(8,128)(2,1)S(1)} %get-tuple-element.75), channel_id=1, source_target_pairs={{0,1},{1,0},{2,3},{3,2},{4,5},{5,4},{6,7},{7,6},{8,9},{9,8},{10,11... | collective-permute-start | bytes 2359304 | tf_op jit(solution)/shard_map/ppermute | solution.py:303
  86.4 2.1 %shard_map.105.row_ref = f32[512,384]{1,0:T(8,128)S(1)} custom-call(bf16[512,384]{1,0:T(8,128)(2,1)S(1)} %copy-done.13, bf16[512,384]{1,0:T(8,128)(2,1)S(1)} %copy-done.15, bf16[512,384]{1,0:T(8,128)(2,1)S(1)} %copy-done.11, f32[1,6]{1,0:T(1,128)S(1)} %bitcast.22), custom_call_target="tpu_custom_call" | custom-call | flops 800000000 | bytes 1966104 | tf_op jit(solution)/shard_map/pallas_call | solution.py:276
  88.5 10.0 %all-to-all-done.1 = bf16[64,8,384]{2,1,0:T(8,128)(2,1)S(1)} async-done(((bf16[64,8,384]{2,1,0:T(8,128)(2,1)}), bf16[64,8,384]{2,1,0:T(8,128)(2,1)S(1)}, u32[]{:S(2)}, u32[]{:S(2)}) %all-to-all-start.1) | async-done | bytes 393248 | tf_op jit(solution)/shard_map/all_to_all | solution.py:321
  99.0 2.1 %collective-permute-start.7 = (bf16[512,384]{1,0:T(8,128)(2,1)S(1)}, bf16[512,384]{1,0:T(8,128)(2,1)S(1)}, u32[]{:S(2)}, u32[]{:S(2)}) collective-permute-start(bf16[512,384]{1,0:T(8,128)(2,1)S(1)} %shard_map.106.gated_ref), channel_id=1, source_target_pairs={{0,1},{1,0},{2,3},{3,2},{4,5},{5,4},{6,7},{7,6},{8,9},{9,8},{10,11... | collective-permute-start | bytes 1179656 | tf_op jit(solution)/shard_map/ppermute | solution.py:303
  101.0 1.7 %collective-permute-done.7.peer_ref = bf16[512,384]{1,0:T(8,128)(2,1)S(1)} collective-permute-done((bf16[512,384]{1,0:T(8,128)(2,1)S(1)}, bf16[512,384]{1,0:T(8,128)(2,1)S(1)}, u32[]{:S(2)}, u32[]{:S(2)}) %collective-permute-start.7) | collective-permute-done | bytes 393248 | tf_op jit(solution)/shard_map/ppermute | solution.py:303
  103.1 1.9 %collective-permute-start.10 = (bf16[512,256]{1,0:T(8,128)(2,1)S(1)}, bf16[512,256]{1,0:T(8,128)(2,1)S(1)}, u32[]{:S(2)}, u32[]{:S(2)}) collective-permute-start(bf16[512,256]{1,0:T(8,128)(2,1)S(1)} %shard_map.109), channel_id=1, source_target_pairs={{0,2},{1,7},{2,4},{3,1},{4,6},{5,3},{6,0},{7,5},{8,10},{9,15},{10,... | collective-permute-start | bytes 786440 | tf_op jit(solution)/shard_map/ppermute | solution.py:299
  106.0 6.0 %collective-permute-start.9 = (bf16[512,256]{1,0:T(8,128)(2,1)S(1)}, bf16[512,256]{1,0:T(8,128)(2,1)S(1)}, u32[]{:S(2)}, u32[]{:S(2)}) collective-permute-start(bf16[512,256]{1,0:T(8,128)(2,1)S(1)} %get-tuple-element.77), channel_id=1, source_target_pairs={{0,6},{1,3},{2,0},{3,5},{4,2},{5,7},{6,4},{7,1},{8,14},{9,11},{10,... | collective-permute-start | bytes 786440 | tf_op jit(solution)/shard_map/ppermute | solution.py:299
  112.1 5.8 %collective-permute-done.10 = bf16[512,256]{1,0:T(8,128)(2,1)S(1)} collective-permute-done((bf16[512,256]{1,0:T(8,128)(2,1)S(1)}, bf16[512,256]{1,0:T(8,128)(2,1)S(1)}, u32[]{:S(2)}, u32[]{:S(2)}) %collective-permute-start.10) | collective-permute-done | bytes 262176 | tf_op jit(solution)/shard_map/ppermute | solution.py:299
  117.9 1.9 %collective-permute-start.11 = (bf16[512,256]{1,0:T(8,128)(2,1)S(1)}, bf16[512,256]{1,0:T(8,128)(2,1)S(1)}, u32[]{:S(2)}, u32[]{:S(2)}) collective-permute-start(bf16[512,256]{1,0:T(8,128)(2,1)S(1)} %add_convert_fusion.1), channel_id=1, source_target_pairs={{0,2},{1,7},{2,4},{3,1},{4,6},{5,3},{6,0},{7,5},{8,10},{9,15},{10,... | collective-permute-start | bytes 786440 | tf_op jit(solution)/shard_map/ppermute | solution.py:299
  119.8 11.2 %collective-permute-done.11 = bf16[512,256]{1,0:T(8,128)(2,1)S(1)} collective-permute-done((bf16[512,256]{1,0:T(8,128)(2,1)S(1)}, bf16[512,256]{1,0:T(8,128)(2,1)S(1)}, u32[]{:S(2)}, u32[]{:S(2)}) %collective-permute-start.11) | collective-permute-done | bytes 262176 | tf_op jit(solution)/shard_map/ppermute | solution.py:299
  (48 shorter events, 6.2 us)
Async XLA Ops:
  1.1 10.3 %copy-start.3 = (bf16[2048,384]{1,0:T(8,128)(2,1)S(1)}, bf16[2048,384]{1,0:T(8,128)(2,1)}, u32[]{:S(2)}) copy-start(bf16[2048,384]{1,0:T(8,128)(2,1)} %refs_1_) | copy-start | bytes 4718596
  1.1 10.3 %copy-start.4 = (bf16[2048,256]{1,0:T(8,128)(2,1)S(1)}, bf16[2048,256]{1,0:T(8,128)(2,1)}, u32[]{:S(2)}) copy-start(bf16[2048,256]{1,0:T(8,128)(2,1)} %refs_2_) | copy-start | bytes 3145732
  1.1 10.3 %copy-start.5 = (bf16[2048,6]{0,1:T(8,128)(2,1)S(1)}, bf16[2048,6]{0,1:T(8,128)(2,1)}, u32[]{:S(2)}) copy-start(bf16[2048,6]{0,1:T(8,128)(2,1)} %param.14) | copy-start | bytes 73732
  1.1 10.3 %copy-start.6 = (f32[2048]{0:T(1024)S(1)}, f32[2048]{0:T(1024)}, u32[]{:S(2)}) copy-start(f32[2048]{0:T(1024)} %param.11) | copy-start | bytes 24580
  1.1 10.3 %copy-start.7 = (f32[6]{0:T(128)S(1)}, f32[6]{0:T(128)}, u32[]{:S(2)}) copy-start(f32[6]{0:T(128)} %param.15) | copy-start | bytes 76
  1.1 10.3 %copy-start.8 = (f32[6]{0:T(128)S(1)}, f32[6]{0:T(128)}, u32[]{:S(2)}) copy-start(f32[6]{0:T(128)} %param.16) | copy-start | bytes 76
  1.1 15.0 %collective-permute-start.1 = (bf16[512,256]{1,0:T(8,128)(2,1)S(1)}, bf16[512,256]{1,0:T(8,128)(2,1)S(1)}, u32[]{:S(2)}, u32[]{:S(2)}) collective-permute-start(bf16[512,256]{1,0:T(8,128)(2,1)S(1)} %bitcast_convert_fusion.x_ref.refs_0_), channel_id=1, source_target_pairs={{0,2},{1,7},{2,4},{3,1},{4,6},{5,3},{6,0},{7,5},{8,10},{9,15},{10,... | collective-permute-start | bytes 786440 | tf_op jit(solution)/shard_map/ppermute | solution.py:299
  4.1 18.3 %collective-permute-start.4 = (bf16[512,256]{1,0:T(8,128)(2,1)S(1)}, bf16[512,256]{1,0:T(8,128)(2,1)S(1)}, u32[]{:S(2)}, u32[]{:S(2)}) collective-permute-start(bf16[512,256]{1,0:T(8,128)(2,1)S(1)} %bitcast_convert_fusion.x_ref.refs_0_), channel_id=1, source_target_pairs={{0,1},{1,0},{2,3},{3,2},{4,5},{5,4},{6,7},{7,6},{8,9},{9,8},{10,11... | collective-permute-start | bytes 786440 | tf_op jit(solution)/shard_map/ppermute | solution.py:303
  6.0 13.9 %collective-permute-start = (bf16[512,256]{1,0:T(8,128)(2,1)S(1)}, bf16[512,256]{1,0:T(8,128)(2,1)S(1)}, u32[]{:S(2)}, u32[]{:S(2)}) collective-permute-start(bf16[512,256]{1,0:T(8,128)(2,1)S(1)} %bitcast_convert_fusion.x_ref.refs_0_), channel_id=1, source_target_pairs={{0,6},{1,3},{2,0},{3,5},{4,2},{5,7},{6,4},{7,1},{8,14},{9,11},{10,... | collective-permute-start | bytes 786440 | tf_op jit(solution)/shard_map/ppermute | solution.py:299
  16.1 6.3 %collective-permute-start.5 = (bf16[512,256]{1,0:T(8,128)(2,1)S(1)}, bf16[512,256]{1,0:T(8,128)(2,1)S(1)}, u32[]{:S(2)}, u32[]{:S(2)}) collective-permute-start(bf16[512,256]{1,0:T(8,128)(2,1)S(1)} %collective-permute-done.1.refs_1_), channel_id=1, source_target_pairs={{0,1},{1,0},{2,3},{3,2},{4,5},{5,4},{6,7},{7,6},{8,9},{9,8},{10,11... | collective-permute-start | bytes 786440 | tf_op jit(solution)/shard_map/ppermute | solution.py:303
  18.0 13.2 %collective-permute-start.2 = (bf16[512,256]{1,0:T(8,128)(2,1)S(1)}, bf16[512,256]{1,0:T(8,128)(2,1)S(1)}, u32[]{:S(2)}, u32[]{:S(2)}) collective-permute-start(bf16[512,256]{1,0:T(8,128)(2,1)S(1)} %collective-permute-done.1.refs_1_), channel_id=1, source_target_pairs={{0,2},{1,7},{2,4},{3,1},{4,6},{5,3},{6,0},{7,5},{8,10},{9,15},{10,... | collective-permute-start | bytes 786440 | tf_op jit(solution)/shard_map/ppermute | solution.py:299
  20.0 11.2 %collective-permute-start.3 = (bf16[512,256]{1,0:T(8,128)(2,1)S(1)}, bf16[512,256]{1,0:T(8,128)(2,1)S(1)}, u32[]{:S(2)}, u32[]{:S(2)}) collective-permute-start(bf16[512,256]{1,0:T(8,128)(2,1)S(1)} %collective-permute-done.refs_0_), channel_id=1, source_target_pairs={{0,1},{1,0},{2,3},{3,2},{4,5},{5,4},{6,7},{7,6},{8,9},{9,8},{10,11... | collective-permute-start | bytes 786440 | tf_op jit(solution)/shard_map/ppermute | solution.py:303
  31.2 3.4 %collective-permute-start.6 = (bf16[512,256]{1,0:T(8,128)(2,1)S(1)}, bf16[512,256]{1,0:T(8,128)(2,1)S(1)}, u32[]{:S(2)}, u32[]{:S(2)}) collective-permute-start(bf16[512,256]{1,0:T(8,128)(2,1)S(1)} %collective-permute-done.2.refs_1_), channel_id=1, source_target_pairs={{0,1},{1,0},{2,3},{3,2},{4,5},{5,4},{6,7},{7,6},{8,9},{9,8},{10,11... | collective-permute-start | bytes 786440 | tf_op jit(solution)/shard_map/ppermute | solution.py:303
  36.8 39.5 %copy-start.10 = (bf16[512,384]{1,0:T(8,128)(2,1)}, bf16[512,384]{1,0:T(8,128)(2,1)S(1)}, u32[]{:S(2)}) copy-start(bf16[512,384]{1,0:T(8,128)(2,1)S(1)} %get-tuple-element.73.inner_ref) | copy-start | bytes 1179652
  36.8 39.4 %copy-start.12 = (bf16[512,384]{1,0:T(8,128)(2,1)}, bf16[512,384]{1,0:T(8,128)(2,1)S(1)}, u32[]{:S(2)}) copy-start(bf16[512,384]{1,0:T(8,128)(2,1)S(1)} %get-tuple-element.71.value_ref) | copy-start | bytes 1179652
  36.8 39.4 %copy-start.14 = (bf16[512,384]{1,0:T(8,128)(2,1)}, bf16[512,384]{1,0:T(8,128)(2,1)S(1)}, u32[]{:S(2)}) copy-start(bf16[512,384]{1,0:T(8,128)(2,1)S(1)} %get-tuple-element.72.side_ref) | copy-start | bytes 1179652
  72.8 11.2 %copy-start = (bf16[384,2048]{1,0:T(8,128)(2,1)S(1)}, bf16[384,2048]{1,0:T(8,128)(2,1)}, u32[]{:S(2)}) copy-start(bf16[384,2048]{1,0:T(8,128)(2,1)} %w_hbm.1) | copy-start | bytes 4718596
  76.3 22.3 %all-to-all-start.1 = ((bf16[64,8,384]{2,1,0:T(8,128)(2,1)}), bf16[64,8,384]{2,1,0:T(8,128)(2,1)S(1)}, u32[]{:S(2)}, u32[]{:S(2)}) async-start(bf16[64,8,384]{2,1,0:T(8,128)(2,1)} %bitcast.7), calls=%async_computation.1 | async-start | bytes 786432 | tf_op jit(solution)/shard_map/all_to_all | solution.py:321
  84.4 14.1 %copy-start.2 = (f32[384]{0:T(512)S(1)}, f32[384]{0:T(512)}, u32[]{:S(2)}) copy-start(f32[384]{0:T(512)} %param.18) | copy-start | bytes 4612
  84.4 16.6 %collective-permute-start.8 = (bf16[384,1024]{1,0:T(8,128)(2,1)S(1)}, bf16[384,1024]{1,0:T(8,128)(2,1)S(1)}, u32[]{:S(2)}, u32[]{:S(2)}) collective-permute-start(bf16[384,1024]{1,0:T(8,128)(2,1)S(1)} %get-tuple-element.75), channel_id=1, source_target_pairs={{0,1},{1,0},{2,3},{3,2},{4,5},{5,4},{6,7},{7,6},{8,9},{9,8},{10,11... | collective-permute-start | bytes 2359304 | tf_op jit(solution)/shard_map/ppermute | solution.py:303
  99.0 3.7 %collective-permute-start.7 = (bf16[512,384]{1,0:T(8,128)(2,1)S(1)}, bf16[512,384]{1,0:T(8,128)(2,1)S(1)}, u32[]{:S(2)}, u32[]{:S(2)}) collective-permute-start(bf16[512,384]{1,0:T(8,128)(2,1)S(1)} %shard_map.106.gated_ref), channel_id=1, source_target_pairs={{0,1},{1,0},{2,3},{3,2},{4,5},{5,4},{6,7},{7,6},{8,9},{9,8},{10,11... | collective-permute-start | bytes 1179656 | tf_op jit(solution)/shard_map/ppermute | solution.py:303
  103.1 14.7 %collective-permute-start.10 = (bf16[512,256]{1,0:T(8,128)(2,1)S(1)}, bf16[512,256]{1,0:T(8,128)(2,1)S(1)}, u32[]{:S(2)}, u32[]{:S(2)}) collective-permute-start(bf16[512,256]{1,0:T(8,128)(2,1)S(1)} %shard_map.109), channel_id=1, source_target_pairs={{0,2},{1,7},{2,4},{3,1},{4,6},{5,3},{6,0},{7,5},{8,10},{9,15},{10,... | collective-permute-start | bytes 786440 | tf_op jit(solution)/shard_map/ppermute | solution.py:299
  106.0 13.8 %collective-permute-start.9 = (bf16[512,256]{1,0:T(8,128)(2,1)S(1)}, bf16[512,256]{1,0:T(8,128)(2,1)S(1)}, u32[]{:S(2)}, u32[]{:S(2)}) collective-permute-start(bf16[512,256]{1,0:T(8,128)(2,1)S(1)} %get-tuple-element.77), channel_id=1, source_target_pairs={{0,6},{1,3},{2,0},{3,5},{4,2},{5,7},{6,4},{7,1},{8,14},{9,11},{10,... | collective-permute-start | bytes 786440 | tf_op jit(solution)/shard_map/ppermute | solution.py:299
  117.9 13.2 %collective-permute-start.11 = (bf16[512,256]{1,0:T(8,128)(2,1)S(1)}, bf16[512,256]{1,0:T(8,128)(2,1)S(1)}, u32[]{:S(2)}, u32[]{:S(2)}) collective-permute-start(bf16[512,256]{1,0:T(8,128)(2,1)S(1)} %add_convert_fusion.1), channel_id=1, source_target_pairs={{0,2},{1,7},{2,4},{3,1},{4,6},{5,3},{6,0},{7,5},{8,10},{9,15},{10,... | collective-permute-start | bytes 786440 | tf_op jit(solution)/shard_map/ppermute | solution.py:299
  (5 other events, 23.3 us)
